TPU v7x, 128 devices: a whole 4x4x4 slice. The times are simulated.
128 devices in a mesh: dp: 16 (over x_lo, z, core), expert: 8 (over y, x_hi).
Axes of the slice: x: 4 (x_hi: 2, x_lo: 2; x = x_hi * 2 + x_lo), y: 4, z: 4, core: 2. Of those that a mesh axis runs over, the one named last changes fastest.
Arguments:
- tokens: bfloat16 [16384, 2048], P(('dp', 'expert')), may hold values from -6 to 6
- norm_gain: float32 [2048], replicated, may hold values from 0.25 to 1.75
- router_weight: bfloat16 [2048, 64], P('dp'), may hold values from -0.25 to 0.25
- expert_ids: int32 [16384, 8], P(('dp', 'expert')), may hold values from 0 to 63, all different within a row; in each aligned block of 128 rows (0 to 127, 128 to 255, ...) at most 32 rows name the same one
- gate_weight: bfloat16 [8, 2048, 1024], P('expert', 'dp'), may hold values from -0.125 to 0.125
- up_weight: bfloat16 [8, 2048, 1024], P('expert', 'dp'), may hold values from -0.125 to 0.125
- down_weight: bfloat16 [8, 2048, 1024], P('expert', 'dp'), may hold values from -0.1875 to 0.1875
- cotangent: bfloat16 [16384, 2048], P(('dp', 'expert')), may hold values from -6 to 6
Outputs:
- mixed: bfloat16 [16384, 2048], P(('dp', 'expert'))
- d_tokens: bfloat16 [16384, 2048], P(('dp', 'expert'))
- d_gain: float32 [2048], replicated
- d_router: float32 [2048, 64], P('dp')
- d_gate: bfloat16 [8, 2048, 1024], P('expert', 'dp')
- d_up: bfloat16 [8, 2048, 1024], P('expert', 'dp')
- d_down: bfloat16 [8, 2048, 1024], P('expert', 'dp')
Inputs may be any that keep to these rules, and one draw needn't show every extreme that they name: `expert_ids`: each row names 8 different experts; in the rows of one device no expert is named more than 32 times.
All inputs are finite; a program needn't handle non-finite values.
Results may differ from a plain program's by a relative error of at most 0.018.
Values may be sent and summed in bfloat16 or wider, within the bound.
No kernel may reach another device: no remote copies, remote signals or barrier semaphores. Data moves between devices by JAX's collectives and lax.ppermute only.
A program may use at most 128 MiB of HBM per device.

v0:
```python
import jax
import jax.numpy as jnp
from jax import lax
from jax.experimental import pallas as pl
from jax.experimental.pallas import tpu as pltpu
from jax.sharding import Mesh
from jax.sharding import PartitionSpec as P


D = 2048
FF = 1024
CAP = 32
TOK = 128
WIN = 8
SLOTS = WIN * CAP
EPSILON = 1e-05
BK = 256
HALF = 512
WIDE = 2 * D + 128
ROWS = 800
CHIPS = 8
F32 = jnp.float32
BF = jnp.bfloat16


def nn(a, b):
    return lax.dot_general(a, b, (((1,), (0,)), ((), ())), preferred_element_type=F32)


def nt(a, b):
    return lax.dot_general(a, b, (((1,), (1,)), ((), ())), preferred_element_type=F32)


def tn(a, b):
    return lax.dot_general(a, b, (((0,), (0,)), ((), ())), preferred_element_type=F32)


def split(v):
    high = v.astype(BF)
    return high, (v - high.astype(F32)).astype(BF)


def sds(shape, dtype):
    return jax.ShapeDtypeStruct(shape, dtype)


SMEM = pl.BlockSpec(memory_space=pltpu.SMEM)
VMEM = pl.BlockSpec(memory_space=pltpu.VMEM)
HBM = pl.BlockSpec(memory_space=pltpu.HBM)


def call(kernel, out_shape, *args, smem=0, near=True, limit=None, scratch=(), far=(), dram=(), far_out=False):
    outs = out_shape if isinstance(out_shape, (list, tuple)) else [out_shape]
    specs = [SMEM] * smem + [VMEM] * (len(args) - smem)
    for i in far:
        specs[i] = HBM
    out_spec = HBM if far_out else VMEM
    if near:
        args = args[:smem] + tuple(
            pltpu.with_memory_space_constraint(v, pltpu.HBM) if i + smem in far or i + smem in dram else pltpu.with_memory_space_constraint(v, pltpu.VMEM)
            for i, v in enumerate(args[smem:])
        )
    params = pltpu.CompilerParams(vmem_limit_bytes=limit) if limit else None
    return pl.pallas_call(
        kernel,
        out_shape=out_shape,
        in_specs=specs,
        out_specs=[out_spec] * len(outs) if isinstance(out_shape, (list, tuple)) else out_spec,
        scratch_shapes=list(scratch),
        compiler_params=params,
    )(*args)


def at(ref_index, block=BK):
    return pl.ds(pl.multiple_of(ref_index, block), block)


def pack_kernel(place, gate, up, down, router_t, away, keep, sems):
    copies = []
    for m, w in enumerate((gate, up, down)):
        for j, (out, side) in enumerate(((away, 1 - place[8]), (keep, place[8]))):
            copies.append(
                pltpu.make_async_copy(
                    w.at[:, at(side * HALF, HALF)], out.at[m * TOK : (m + 1) * TOK, :], sems.at[j, m]
                )
            )
    for c in copies:
        c.start()
    for g in range(4):
        for out in (away, keep):
            out[384:400, g * TOK : (g + 1) * TOK] = router_t[g * 16 : (g + 1) * 16, :]
    for c in copies:
        c.wait()


def join_kernel(place, keep, other, own):
    core = place[8]
    for source, side in ((keep, core), (other, 1 - core)):
        for m in range(3):
            own[at(m * BK + side * TOK, TOK), :] = source[m * TOK : (m + 1) * TOK, :]
        own[at(768 + side * 16, 16), :] = source[384:400, :]


def router_rows(piece, c):
    rows = piece[768 + c * 16 : 784 + c * 16, :]
    return jnp.concatenate([rows[:, g * TOK : (g + 1) * TOK] for g in range(4)], axis=0)


def dispatch_kernel(place, tokens, cotangent, gain, ids, hidden, xs, gains, root, spread, chosen, outgoing):
    lane = lax.broadcasted_iota(jnp.int32, (TOK, 128), 1)
    picked = jnp.zeros((TOK, 128), F32)
    for k in range(8):
        picked = picked + (ids[:, k : k + 1] == lane).astype(F32)
    chosen[...] = picked
    half = picked.astype(BF)
    row = lax.broadcasted_iota(jnp.int32, (TOK, TOK), 0)
    col = lax.broadcasted_iota(jnp.int32, (TOK, TOK), 1)
    earlier = nn((col < row).astype(F32).astype(BF), half)
    who = lax.broadcasted_iota(jnp.int32, (128, SLOTS), 0)
    slot = lax.broadcasted_iota(jnp.int32, (128, SLOTS), 1)
    widen = (who == slot // CAP).astype(F32).astype(BF)
    position = nn(earlier.astype(BF), widen)
    named = nn(half, widen)
    column = lax.broadcasted_iota(jnp.int32, (TOK, SLOTS), 1)
    table = jnp.where(
        (named > 0.5) & (position == (column % CAP).astype(F32)), 1.0, 0.0
    ).astype(BF)
    spread[...] = table
    total = jnp.zeros((TOK, 1), F32)
    for b in range(CHIPS):
        x = tokens[:, at(place[b] * BK)]
        xs[:, b * BK : (b + 1) * BK] = x
        x = x.astype(F32)
        total = total + jnp.sum(x * x, axis=-1, keepdims=True)
    r = lax.rsqrt(total * (1.0 / D) + EPSILON)
    root[...] = jnp.broadcast_to(r, (TOK, 128))
    for b in range(CHIPS):
        cols = slice(b * BK, (b + 1) * BK)
        g = gain[:, at(place[b] * BK)]
        gains[:, cols] = g
        h = (xs[:, cols].astype(F32) * r * g).astype(BF)
        hidden[:, cols] = h
        outgoing[:, cols] = tn(table, h).astype(BF)
        outgoing[:, D + b * BK : D + (b + 1) * BK] = tn(
            table, cotangent[:, at(place[b] * BK)]
        ).astype(BF)
    outgoing[:, 2 * D :] = tn(table, half).astype(BF)


def flip_kernel(mine, other, flipped):
    for b in range(16):
        cols = slice(b * BK, (b + 1) * BK)
        flipped[cols, 0:SLOTS] = mine[:, cols].T
        flipped[cols, SLOTS : 2 * SLOTS] = other[:, cols].T


EARLY = (0, 1, 3, 4, 2, 5)
LATE = (7, 6)


def products(rows, pieces, blocks, totals, logits):
    for b, piece in zip(blocks, pieces):
        x = rows[:, b * BK : (b + 1) * BK]
        y = rows[:, D + b * BK : D + (b + 1) * BK]
        totals[0] = totals[0] + nn(x, piece[0:256, :])
        totals[1] = totals[1] + nn(x, piece[256:512, :])
        totals[2] = totals[2] + nn(y, piece[512:768, :])
        for c in range(2):
            logits = logits + nt(x[:, c * TOK : (c + 1) * TOK], router_rows(piece, c))
    return totals, logits


def fetch(sources, held, sems):
    copies = [
        pltpu.make_async_copy(source, held.at[n], sems.at[n]) for n, source in enumerate(sources)
    ]
    for c in copies:
        c.start()
    for c in copies:
        c.wait()
    return [held.at[n] for n in range(len(copies))]


def keep_products(rows, pieces, sums, slot_logits):
    totals, logits = products(
        rows, pieces, EARLY, [jnp.zeros((SLOTS, HALF), F32)] * 3, jnp.zeros((SLOTS, 64), F32)
    )
    for m in range(3):
        sums[:, m * HALF : (m + 1) * HALF] = totals[m]
    slot_logits[...] = logits


def early_kernel(rows, *refs):
    sums, slot_logits, routed, held, sems = refs[6:]
    pieces = fetch(refs[:6], held, sems)
    keep_products(rows, pieces, sums, slot_logits)
    for n in range(6):
        for c in range(2):
            routed[:, (2 * n + c) * TOK : (2 * n + c + 1) * TOK] = router_rows(pieces[n], c)


def early_other_kernel(rows, held, sums, slot_logits):
    keep_products(rows, [held.at[n] for n in range(6)], sums, slot_logits)


def late_kernel(place, *refs):
    act, scaled, grad_gate, grad_up, routed, held, sems = refs[8:]
    pieces = fetch(refs[6:8], held, sems)
    lane = lax.broadcasted_iota(jnp.int32, (SLOTS, 64), 1)
    for i in range(2):
        rows, sums, slot_logits = refs[3 * i : 3 * i + 3]
        out = slice(i * SLOTS, (i + 1) * SLOTS)
        totals, logits = products(
            rows, pieces, LATE, [sums[:, m * HALF : (m + 1) * HALF] for m in range(3)],
            slot_logits[...],
        )
        picked = rows[:, 2 * D : 2 * D + 64].astype(F32) > 0.5
        raised = jnp.where(picked, jnp.exp(logits), 0.0)
        mine = jnp.sum(jnp.where(lane == place[9], raised, 0.0), axis=-1, keepdims=True)
        total = jnp.sum(raised, axis=-1, keepdims=True)
        w = jnp.where(total > 0.0, mine / jnp.where(total > 0.0, total, 1.0), 0.0)
        gate, up, back = totals
        sig = jax.nn.sigmoid(gate)
        silu = gate * sig
        active = silu * up
        back = back * w
        act[out, :] = active.astype(BF)
        scaled[out, :] = (active * w).astype(BF)
        grad_gate[out, :] = (back * up * sig * (1.0 + gate * (1.0 - sig))).astype(BF)
        grad_up[out, :] = (back * silu).astype(BF)
    for n in range(2):
        for c in range(2):
            routed[:, (2 * n + c) * TOK : (2 * n + c + 1) * TOK] = router_rows(pieces[n], c)


def output_kernel(i):
    def kernel(rows, act, grad_gate, grad_up, first, last, out, gain):
        some = slice(i * SLOTS, (i + 1) * SLOTS)
        for b in range(CHIPS):
            cols = slice(b * BK, (b + 1) * BK)
            piece = first.at[EARLY.index(b)] if b in EARLY else last.at[LATE.index(b)]
            out[:, cols] = nt(act[some, :], piece[512:768, :]).astype(BF)
            total = nt(grad_gate[some, :], piece[0:256, :])
            total = total + nt(grad_up[some, :], piece[256:512, :])
            out[:, D + b * BK : D + (b + 1) * BK] = total.astype(BF)
            gain[:, cols] = jnp.sum(total * rows[:, cols].astype(F32), axis=0, keepdims=True)

    return kernel


def grads_kernel(blocks):
    def kernel(flipped, scaled, grad_gate, grad_up, *refs):
        outs, stage, sems = refs[:-2], refs[-2], refs[-1]
        copies = {}
        for n, b in enumerate(blocks):
            slot = n % 3
            if n >= 3:
                copies[n - 3].wait()
            x = flipped[b * BK : (b + 1) * BK, :]
            stage[slot, 0:256, :] = nn(x, grad_gate[...]).astype(BF)
            stage[slot, 256:512, :] = nn(x, grad_up[...]).astype(BF)
            stage[slot, 512:768, :] = nn(
                flipped[D + b * BK : D + (b + 1) * BK, :], scaled[...]
            ).astype(BF)
            copies[n] = pltpu.make_async_copy(stage.at[slot], outs[n], sems.at[slot])
            copies[n].start()
        for n in range(max(0, len(blocks) - 3), len(blocks)):
            copies[n].wait()

    return kernel


def block_of(routed_early, routed_late, b):
    source, n = (routed_early, EARLY.index(b)) if b in EARLY else (routed_late, LATE.index(b))
    return source[:, n * BK : (n + 1) * BK]


def pick_weights(hidden, routed_early, routed_late, chosen):
    logits = jnp.zeros((TOK, 64), F32)
    for b in range(CHIPS):
        r = block_of(routed_early, routed_late, b)
        logits = logits + nt(hidden[:, b * BK : (b + 1) * BK], r)
    raised = jnp.where(chosen[:, :64] > 0.5, jnp.exp(logits), 0.0)
    return raised / jnp.sum(raised, axis=-1, keepdims=True)


def mix_kernel(place, returned, cotangent, spread, chosen, hidden, routed_early, routed_late, gains, gain_mine, gain_other, weight, grad_logits, parts, work):
    w = pick_weights(hidden, routed_early, routed_late, chosen)
    weight[...] = w
    per_slot = jnp.zeros((SLOTS, 1), F32)
    for b in range(CHIPS):
        c = tn(spread[...], cotangent[:, at(place[b] * BK)])
        y = returned[:, b * BK : (b + 1) * BK].astype(F32)
        per_slot = per_slot + jnp.sum(c * y, axis=-1, keepdims=True)
    slot = lax.broadcasted_iota(jnp.int32, (SLOTS, 64), 0)
    who = lax.broadcasted_iota(jnp.int32, (SLOTS, 64), 1)
    spots = jnp.where(who == slot // CAP, per_slot, 0.0)
    high = spots.astype(BF)
    rest = spots - high.astype(F32)
    middle = rest.astype(BF)
    low = (rest - middle.astype(F32)).astype(BF)
    table = spread[...]
    grad_weights = nn(table, high) + nn(table, middle) + nn(table, low)
    inner = jnp.sum(w * grad_weights, axis=-1, keepdims=True)
    g = w * (grad_weights - inner)
    grad_logits[...] = g
    gh, gl = split(g)
    for b in range(CHIPS):
        cols = slice(b * BK, (b + 1) * BK)
        h = hidden[:, cols]
        part = tn(gh, h) + tn(gl, h)
        gain = gain_mine[:, cols] + gain_other[:, cols] + jnp.sum(
            part * block_of(routed_early, routed_late, b).astype(F32), axis=0, keepdims=True
        )
        gain_high, gain_low = split(gain / gains[:, cols])
        for c in range(2):
            home = place[b] * 2 + c
            lanes = slice(c * TOK, (c + 1) * TOK)
            parts[home, 0:64, :] = part[:, lanes].astype(BF)
            work[pl.ds(home, 1), :] = gain_high[:, lanes].astype(F32)
            work[pl.ds(16 + home, 1), :] = gain_low[:, lanes].astype(F32)
    whole = work[...].astype(BF)
    for d in range(16):
        parts[d, 64:96, :] = whole


def norm_kernel(place, returned, spread, weight, grad_logits, routed_early, routed_late, xs, gains, root, mixed, d_tokens, work):
    who = lax.broadcasted_iota(jnp.int32, (64, SLOTS), 0)
    slot = lax.broadcasted_iota(jnp.int32, (64, SLOTS), 1)
    widen = (who == slot // CAP).astype(F32).astype(BF)
    high, low = split(weight[...])
    table = spread[...]
    mask = table.astype(F32)
    blend_high = (nn(high, widen) * mask).astype(BF)
    blend_low = (nn(low, widen) * mask).astype(BF)
    gh, gl = split(grad_logits[...])
    r = root[:, 0:1]
    inner = jnp.zeros((TOK, 1), F32)
    for b in range(CHIPS):
        cols = slice(b * BK, (b + 1) * BK)
        y = returned[:, cols]
        mixed[:, at(place[b] * BK)] = (nn(blend_high, y) + nn(blend_low, y)).astype(BF)
        rt = block_of(routed_early, routed_late, b)
        grad = nn(table, returned[:, D + b * BK : D + (b + 1) * BK]) + nn(gh, rt) + nn(gl, rt)
        scaled = grad * gains[:, cols]
        work[:, cols] = scaled
        inner = inner + jnp.sum(scaled * xs[:, cols].astype(F32), axis=-1, keepdims=True)
    factor = inner * (r * r * r) * (1.0 / D)
    for b in range(CHIPS):
        cols = slice(b * BK, (b + 1) * BK)
        d_tokens[:, at(place[b] * BK)] = (
            work[:, cols] * r - xs[:, cols].astype(F32) * factor
        ).astype(BF)


def total_kernel(place, here, ahead, behind, left, right, give, keep):
    core = place[8]
    for m in range(3):
        for out, side in ((give, 1 - core), (keep, core)):
            rows = at(m * BK + side * TOK, TOK)
            for h, last in enumerate((left, right)):
                cols = slice(h * BK, (h + 1) * BK)
                total = here[rows, cols].astype(F32) + ahead[rows, cols].astype(F32)
                total = total + behind[rows, cols].astype(F32) + last[rows, :].astype(F32)
                out[m * TOK : (m + 1) * TOK, cols] = total.astype(BF)


def share_kernel(parts, shares):
    total = parts[0].astype(F32)
    for d in range(1, 16):
        total = total + parts[d].astype(F32)
    for e in range(WIN):
        shares[e, 0:64, :] = total[0:64]
        shares[e, 64:80, :] = total[64:80] + total[80:96]


def small_kernel(shares, d_router, d_gain):
    total = shares[0]
    for e in range(1, WIN):
        total = total + shares[e]
    d_router[...] = total[0:64]
    d_gain[...] = total[64:80]


def finish_kernel(place, keep, other, *outs):
    core = place[8]
    for m, out in enumerate(outs):
        rows = slice(m * TOK, (m + 1) * TOK)
        out[:, at(core * HALF, HALF)] = keep[rows, :]
        out[:, at((1 - core) * HALF, HALF)] = other[rows, :]


def perm(move):
    pairs = []
    for x in range(2):
        for z in range(4):
            for c in range(2):
                tx, tz, tc = move(x, z, c)
                pairs.append(((x * 4 + z) * 2 + c, (tx * 4 + tz % 4) * 2 + tc))
    return pairs


SIBLING = perm(lambda x, z, c: (x, z, 1 - c))
ACROSS = perm(lambda x, z, c: (1 - x, z, c))
AHEAD = perm(lambda x, z, c: (x, z + 1, c))
BEHIND = perm(lambda x, z, c: (x, z + 3, c))


DP = ("chip", "core")


def send(v, pairs):
    return lax.ppermute(v, DP, pairs)


def gather_pieces(own):
    across = send(own, ACROSS)
    own_1 = send(own, BEHIND)
    own_3 = send(own, AHEAD)
    across_1 = send(across, BEHIND)
    across_3 = send(across, AHEAD)
    own_2 = send(own_3, AHEAD)
    across_2 = send(across_1, BEHIND)
    return (own, own_1, own_2, own_3, across, across_1, across_2, across_3)


def plus(*values):
    total = values[0].astype(F32)
    for v in values[1:]:
        total = total + v.astype(F32)
    return total.astype(BF)


def reduce_pieces(parts):
    cols = [slice(h * BK, (h + 1) * BK) for h in range(2)]
    across_2 = send(parts[6], BEHIND)
    own_2 = send(parts[2], AHEAD)
    across_1 = send(parts[5], AHEAD)
    across_3 = [send(plus(parts[7][:, cols[h]], across_2[:, cols[h]]), BEHIND) for h in range(2)]
    own_3 = send(parts[3], BEHIND)
    own_1 = send(plus(parts[1], own_2), AHEAD)
    across = [send(plus_half(h, parts[4], across_1, across_3[h]), ACROSS) for h in range(2)]
    return parts[0], own_1, own_3, *across


def sum_kernel(h):
    def kernel(*refs):
        sources, out, stage, sems = refs[:-3], refs[-3], refs[-2], refs[-1]
        copies = []
        for n, source in enumerate(sources):
            if source.shape[1] != BK:
                source = source.at[:, h * BK : (h + 1) * BK]
            copies.append(pltpu.make_async_copy(source, stage.at[n], sems.at[n]))
            copies[n].start()
        for c in copies:
            c.wait()
        total = stage[0].astype(F32)
        for n in range(1, len(copies)):
            total = total + stage[n].astype(F32)
        out[...] = total.astype(BF)

    return kernel


def plus_half(h, *values):
    count = len(values)
    return call(
        sum_kernel(h), sds((768, BK), BF), *values, far=range(count), limit=MiB(3),
        scratch=[pltpu.VMEM((count, 768, BK), BF), pltpu.SemaphoreType.DMA((count,))],
    )


def exchange(v, axis):
    return lax.all_to_all(v, axis, split_axis=0, concat_axis=0, tiled=True)


def body(
    tokens, norm_gain, router_weight, expert_ids, gate_weight, up_weight, down_weight, cotangent
):
    chip = lax.axis_index("chip")
    core = lax.axis_index("core")
    x, z = chip >> 2, chip & 3
    rel = jnp.arange(16, dtype=jnp.int32)
    chips = ((x ^ ((rel >> 2) & 1)) * 4 + ((z + rel) & 3)).astype(jnp.int32)
    mine = jnp.where(rel == 8, core, lax.axis_index("expert")).astype(jnp.int32)
    place = jnp.where(rel < 8, chips, mine)

    weights = (gate_weight[0], up_weight[0], down_weight[0])
    away, keep_own = call(
        pack_kernel, [sds((400, HALF), BF)] * 2, place, *weights, router_weight.T, smem=1,
        limit=MiB(2), far=(1, 2, 3), scratch=[pltpu.SemaphoreType.DMA((2, 3))],
    )
    other = send(away, SIBLING)
    hidden, xs, gains, root, spread, chosen, sent = call(
        dispatch_kernel,
        [pltpu.HBM((TOK, D), BF), pltpu.HBM((TOK, D), BF), pltpu.HBM((1, D), F32),
         pltpu.HBM((TOK, 128), F32), pltpu.HBM((TOK, SLOTS), BF), pltpu.HBM((TOK, 128), F32),
         pltpu.HBM((SLOTS, WIDE), BF)],
        place, tokens, cotangent, norm_gain[None], expert_ids, smem=1, dram=(1, 2, 3),
        limit=MiB(12),
    )
    own = call(join_kernel, sds((ROWS, HALF), BF), place, keep_own, other, smem=1, limit=MiB(3))
    pieces = gather_pieces(own)

    rows = exchange(sent.reshape(WIN, CAP, WIDE), "expert").reshape(SLOTS, WIDE)
    rows_other = send(rows, SIBLING)
    flipped = call(flip_kernel, sds((2 * D, 2 * SLOTS), BF), rows, rows_other, limit=MiB(12))
    shapes = [sds((SLOTS, 3 * HALF), F32), sds((SLOTS, 64), F32)]
    sums, slot_logits, routed_early, held_early = call(
        early_kernel,
        shapes + [pltpu.HBM((64, 6 * BK), BF), pltpu.VMEM((6, ROWS, HALF), BF)],
        rows, *[pieces[b] for b in EARLY], limit=MiB(6), far=range(1, 7),
        scratch=[pltpu.SemaphoreType.DMA((6,))],
    )
    sums_other, logits_other = call(
        early_other_kernel, shapes, rows_other, held_early, limit=MiB(6),
    )
    act, scaled, grad_gate, grad_up, routed_late, held_late = call(
        late_kernel,
        [sds((2 * SLOTS, HALF), BF)] * 4
        + [pltpu.HBM((64, 2 * BK), BF), pltpu.VMEM((2, ROWS, HALF), BF)],
        place, rows, sums, slot_logits, rows_other, sums_other, logits_other,
        *[pieces[b] for b in LATE], smem=1, limit=MiB(8), far=(7, 8),
        scratch=[pltpu.SemaphoreType.DMA((2,))],
    )
    (partial_other, gain_other), (partial, gain_mine) = (
        call(
            output_kernel(i), [sds((SLOTS, 2 * D), BF), sds((1, D), F32)],
            source, act, grad_gate, grad_up, held_early, held_late, limit=MiB(6),
        )
        for i, source in ((1, rows_other), (0, rows))
    )
    output = plus(partial, send(partial_other, SIBLING))
    returned = exchange(output.reshape(WIN, CAP, 2 * D), "expert")
    returned = returned.reshape(SLOTS, 2 * D)
    parts = {}
    for blocks in ((6, 2, 5), (7, 3, 1, 4, 0)):
        made = call(
            grads_kernel(blocks), [pltpu.HBM((768, HALF), BF)] * len(blocks),
            flipped, scaled, grad_gate, grad_up, limit=MiB(5), far_out=True,
            scratch=[pltpu.VMEM((3, 768, HALF), BF), pltpu.SemaphoreType.DMA((3,))],
        )
        parts.update(zip(blocks, made))
    give, keep = call(
        total_kernel, [sds((384, HALF), BF)] * 2, place, *reduce_pieces(parts),
        smem=1, limit=MiB(6),
    )
    fetched = send(give, SIBLING)
    d_weights = call(
        finish_kernel, [pltpu.HBM((TOK, FF), BF)] * 3, place, keep, fetched,
        smem=1, limit=MiB(4),
    )

    weight, grad_logits, shares = call(
        mix_kernel,
        [sds((TOK, 64), F32), sds((TOK, 64), F32), pltpu.HBM((16, 96, TOK), BF)],
        place, returned, cotangent, spread, chosen, hidden, routed_early, routed_late, gains,
        gain_mine, gain_other, smem=1, dram=range(2, 9), limit=MiB(12),
        scratch=[pltpu.VMEM((32, TOK), F32)],
    )
    shares = exchange(shares, DP)
    shares = call(share_kernel, sds((8, 80, TOK), F32), shares, limit=MiB(2))
    shares = exchange(shares, "expert")
    d_router, d_gain = call(
        small_kernel, [pltpu.HBM((64, TOK), F32), pltpu.HBM((16, TOK), F32)], shares, limit=MiB(2)
    )

    mixed, d_tokens = call(
        norm_kernel, [pltpu.HBM((TOK, D), BF)] * 2,
        place, returned, spread, weight, grad_logits, routed_early, routed_late, xs, gains, root,
        smem=1, dram=(2, 5, 6, 7, 8, 9), limit=MiB(10), scratch=[pltpu.VMEM((TOK, D), F32)],
    )
    return (mixed, d_tokens, d_gain.reshape(D), d_router.T, *[d[None] for d in d_weights])


def MiB(n):
    return n << 20


def solution(mesh):
    grid = Mesh(mesh.devices.reshape(8, 2, 8), ("chip", "core", "expert"))
    every = P(("chip", "core", "expert"), None)
    rows = P("expert", DP, None)
    in_specs = (every, P(), P(DP, None), every, rows, rows, rows, every)
    out_specs = (every, every, P(), P(DP, None), rows, rows, rows)
    return jax.shard_map(body, mesh=grid, in_specs=in_specs, out_specs=out_specs, check_vma=False)
```

profile of v0, /device:TPU:1, one launch (start us, length us, event | category | flops | bytes accessed | tf_op | source)
XLA Modules:
  0.0 220.3 jit_solution(283791727150208978)
XLA Ops:
  1.4 4.0 %shard_map.135 = (bf16[128,2048]{1,0:T(8,128)(2,1)}, bf16[128,2048]{1,0:T(8,128)(2,1)}, f32[1,2048]{1,0:T(1,128)}, f32[128,128]{1,0:T(8,128)}, bf16[128,256]{1,0...) custom-call(s32[16]{0:T(128)S(1)} %compare_select_fusion.1.place, bf16[128,2048]{1,0:T(8,128)(2,1)} %tokens.1, ...), custom_call_target="tpu_custom_call" | custom-call | tf_op jit(solution)/shard_map/pallas_call | solution.py:64
  5.5 7.6 %all-to-all-start = ((bf16[8,32,4224]{2,1,0:T(8,128)(2,1)}), bf16[8,32,4224]{2,1,0:T(8,128)(2,1)S(1)}, u32[]{:S(2)}, u32[]{:S(2)}) async-start(bf16[8,32,4224]{2,1,0:T(8,128)(2,1)} %bitcast.23), calls=%async_computation | async-start | bytes 4325376 | tf_op jit(solution)/shard_map/all_to_all | solution.py:474
  18.3 23.0 %all-to-all-done = bf16[8,32,4224]{2,1,0:T(8,128)(2,1)S(1)} async-done(((bf16[8,32,4224]{2,1,0:T(8,128)(2,1)}), bf16[8,32,4224]{2,1,0:T(8,128)(2,1)S(1)}, u32[]{:S(2)}, u32[]{:S(2)}) %all-to-all-start) | async-done | bytes 2162720 | tf_op jit(solution)/shard_map/all_to_all | solution.py:474
  41.3 3.2 %collective-permute-start.6 = (bf16[256,4224]{1,0:T(8,128)(2,1)S(1)}, bf16[256,4224]{1,0:T(8,128)(2,1)S(1)}, u32[]{:S(2)}, u32[]{:S(2)}) collective-permute-start(bf16[256,4224]{1,0:T(8,128)(2,1)S(1)} %bitcast.14), channel_id=1, source_target_pairs={{0,8},{8,0},{16,24},{24,16},{32,40},{40,32},{48,56},{56,48},{64,72... | collective-permute-start | bytes 6488072 | tf_op jit(solution)/shard_map/ppermute | solution.py:413
  46.2 8.5 %collective-permute-done.3.refs_3_ = bf16[800,512]{1,0:T(8,128)(2,1)} collective-permute-done((bf16[800,512]{1,0:T(8,128)(2,1)S(1)}, bf16[800,512]{1,0:T(8,128)(2,1)}, u32[]{:S(2)}, u32[]{:S(2)}) %collective-permute-start.3) | collective-permute-done | bytes 819232 | tf_op jit(solution)/shard_map/ppermute | solution.py:413
  54.7 3.8 %collective-permute-start.5 = (bf16[800,512]{1,0:T(8,128)(2,1)}, bf16[800,512]{1,0:T(8,128)(2,1)S(1)}, u32[]{:S(2)}, u32[]{:S(2)}) collective-permute-start(bf16[800,512]{1,0:T(8,128)(2,1)} %collective-permute-done.3.refs_3_), channel_id=1, source_target_pairs={{0,48},{8,56},{16,0},{24,8},{32,16},{40,24},{48,32},{56,40},{64,11... | collective-permute-start | bytes 2457608 | tf_op jit(solution)/shard_map/ppermute | solution.py:413
  58.6 8.4 %collective-permute-done.2.refs_2_ = bf16[800,512]{1,0:T(8,128)(2,1)S(1)} collective-permute-done((bf16[800,512]{1,0:T(8,128)(2,1)S(1)}, bf16[800,512]{1,0:T(8,128)(2,1)S(1)}, u32[]{:S(2)}, u32[]{:S(2)}) %collective-permute-start.2) | collective-permute-done | bytes 819232 | tf_op jit(solution)/shard_map/ppermute | solution.py:413
  67.7 7.2 %collective-permute-done.5.refs_5_ = bf16[800,512]{1,0:T(8,128)(2,1)S(1)} collective-permute-done((bf16[800,512]{1,0:T(8,128)(2,1)}, bf16[800,512]{1,0:T(8,128)(2,1)S(1)}, u32[]{:S(2)}, u32[]{:S(2)}) %collective-permute-start.5) | collective-permute-done | bytes 819232 | tf_op jit(solution)/shard_map/ppermute | solution.py:413
  74.8 3.3 %collective-permute-start.8 = (bf16[800,512]{1,0:T(8,128)(2,1)S(1)}, bf16[800,512]{1,0:T(8,128)(2,1)S(1)}, u32[]{:S(2)}, u32[]{:S(2)}) collective-permute-start(bf16[800,512]{1,0:T(8,128)(2,1)S(1)} %collective-permute-done.5.refs_5_), channel_id=1, source_target_pairs={{0,48},{8,56},{16,0},{24,8},{32,16},{40,24},{48,32},{56,40},{64,11... | collective-permute-start | bytes 2457608 | tf_op jit(solution)/shard_map/ppermute | solution.py:413
  78.1 14.1 %collective-permute-done.1.refs_1_ = bf16[800,512]{1,0:T(8,128)(2,1)S(1)} collective-permute-done((bf16[800,512]{1,0:T(8,128)(2,1)S(1)}, bf16[800,512]{1,0:T(8,128)(2,1)S(1)}, u32[]{:S(2)}, u32[]{:S(2)}) %collective-permute-start.1) | collective-permute-done | bytes 819232 | tf_op jit(solution)/shard_map/ppermute | solution.py:413
  94.2 4.7 %shard_map.138 = (f32[256,1536]{1,0:T(8,128)S(1)}, f32[256,64]{1,0:T(8,128)S(1)}, bf16[64,1536]{1,0:T(8,128)(2,1)}, bf16[6,800,512]{2,1,0:T(8,128)(2,1)S(1)}) custom-call(bf16[256,4224]{1,0:T(8,128)(2,1)S(1)} %bitcast.15, bf16[800,512]{1,0:T(8,128)(2,1)} %copy-done.2, bf16[800,512]{1,0:T(8,128)(2,1)} %copy-done.14, bf16[800,512]{1,0:T(8,128)(2,1)} %copy-done.12, ...), custom_call_target="tpu_custom_call" | custom-call | tf_op jit(solution)/shard_map/pallas_call | solution.py:64
  100.4 4.5 %collective-permute-done.7.refs_6_ = bf16[800,512]{1,0:T(8,128)(2,1)S(1)} collective-permute-done((bf16[800,512]{1,0:T(8,128)(2,1)}, bf16[800,512]{1,0:T(8,128)(2,1)S(1)}, u32[]{:S(2)}, u32[]{:S(2)}) %collective-permute-start.7) | collective-permute-done | bytes 819232 | tf_op jit(solution)/shard_map/ppermute | solution.py:413
  104.9 4.9 %collective-permute-done.8.refs_7_ = bf16[800,512]{1,0:T(8,128)(2,1)S(1)} collective-permute-done((bf16[800,512]{1,0:T(8,128)(2,1)S(1)}, bf16[800,512]{1,0:T(8,128)(2,1)S(1)}, u32[]{:S(2)}, u32[]{:S(2)}) %collective-permute-start.8) | collective-permute-done | bytes 819232 | tf_op jit(solution)/shard_map/ppermute | solution.py:413
  110.7 4.4 %shard_map.140 = (bf16[512,512]{1,0:T(8,128)(2,1)S(1)}, bf16[512,512]{1,0:T(8,128)(2,1)S(1)}, bf16[512,512]{1,0:T(8,128)(2,1)S(1)}, bf16[512,512]{1,0:T(8,128)(2...) custom-call(s32[16]{0:T(128)S(1)} %compare_select_fusion.1.place, bf16[256,4224]{1,0:T(8,128)(2,1)S(1)} %bitcast.16, ...), custom_call_target="tpu_custom_call" | custom-call | tf_op jit(solution)/shard_map/pallas_call | solution.py:64
  125.6 3.5 %collective-permute-start.14 = (bf16[768,512]{1,0:T(8,128)(2,1)}, bf16[768,512]{1,0:T(8,128)(2,1)}, u32[]{:S(2)}, u32[]{:S(2)}) collective-permute-start(bf16[768,512]{1,0:T(8,128)(2,1)} %get-tuple-element.91), channel_id=1, source_target_pairs={{0,48},{8,56},{16,0},{24,8},{32,16},{40,24},{48,32},{56,40},{64,11... | collective-permute-start | bytes 2359304 | tf_op jit(solution)/shard_map/ppermute | solution.py:413
  131.2 7.4 %all-to-all-start.1 = ((bf16[8,32,4096]{2,1,0:T(8,128)(2,1)}), bf16[8,32,4096]{2,1,0:T(8,128)(2,1)S(1)}, u32[]{:S(2)}, u32[]{:S(2)}) async-start(bf16[8,32,4096]{2,1,0:T(8,128)(2,1)} %bitcast.22), calls=%async_computation.1 | async-start | bytes 4194304 | tf_op jit(solution)/shard_map/all_to_all | solution.py:474
  141.9 3.6 %shard_map.148 = (bf16[768,512]{1,0:T(8,128)(2,1)}, bf16[768,512]{1,0:T(8,128)(2,1)}, bf16[768,512]{1,0:T(8,128)(2,1)}, bf16[768,512]{1,0:T(8,128)(2,1)}, bf16[768,512]{1,0:T(8,128)(2,1)}) custom-call(bf16[4096,512]{1,0:T(8,128)(2,1)S(1)} %copy-done.1, bf16[512,512]{1,0:T(8,128)(2,1)S(1)} %copy-done.4, bf16[512,512]{1,0:T(8,128)(2,1)S(1)} %get-tuple-element.61.grad_gate, ...), custom_call_target="tpu_custom_call" | custom-call | tf_op jit(solution)/shard_map/pallas_call | solution.py:64
  151.3 7.3 %collective-permute-done.10 = bf16[768,512]{1,0:T(8,128)(2,1)S(1)} collective-permute-done((bf16[768,512]{1,0:T(8,128)(2,1)}, bf16[768,512]{1,0:T(8,128)(2,1)S(1)}, u32[]{:S(2)}, u32[]{:S(2)}) %collective-permute-start.10) | collective-permute-done | bytes 786464 | tf_op jit(solution)/shard_map/ppermute | solution.py:413
  162.4 13.1 %collective-permute-done.13.refs_1_ = bf16[768,512]{1,0:T(8,128)(2,1)S(1)} collective-permute-done((bf16[768,512]{1,0:T(8,128)(2,1)S(1)}, bf16[768,512]{1,0:T(8,128)(2,1)S(1)}, u32[]{:S(2)}, u32[]{:S(2)}) %collective-permute-start.13) | collective-permute-done | bytes 786464 | tf_op jit(solution)/shard_map/ppermute | solution.py:413
  184.4 3.5 %shard_map.143 = (f32[128,64]{1,0:T(8,128)S(1)}, f32[128,64]{1,0:T(8,128)S(1)}, bf16[16,96,128]{2,1,0:T(8,128)(2,1)}) custom-call(s32[16]{0:T(128)S(1)} %compare_select_fusion.1.place, bf16[256,4096]{1,0:T(8,128)(2,1)S(1)} %bitcast.19, bf16[128,2048]{1,0:T(8,128)(2,1)} %cotangent.3, bf16[128,256]{1,0:T(8,128)(2,1)} %get-tuple-element.66.spread, ...), custom_call_target="tpu_custom_call" | custom-call | tf_op jit(solution)/shard_map/pallas_call | solution.py:64
  187.9 8.1 %all-to-all-start.2 = ((bf16[16,96,128]{2,1,0:T(8,128)(2,1)}), bf16[16,96,128]{2,1,0:T(8,128)(2,1)S(1)}, u32[]{:S(2)}, u32[]{:S(2)}) async-start(bf16[16,96,128]{2,1,0:T(8,128)(2,1)} %get-tuple-element.80), calls=%async_computation.2 | async-start | bytes 786432 | tf_op jit(solution)/shard_map/all_to_all | solution.py:474
  199.5 2.9 %collective-permute-start.19 = (bf16[384,512]{1,0:T(8,128)(2,1)}, bf16[384,512]{1,0:T(8,128)(2,1)S(1)}, u32[]{:S(2)}, u32[]{:S(2)}) collective-permute-start(bf16[384,512]{1,0:T(8,128)(2,1)} %get-tuple-element.93), channel_id=1, source_target_pairs={{0,8},{8,0},{16,24},{24,16},{32,40},{40,32},{48,56},{56,48},{64,72... | collective-permute-start | bytes 1179656 | tf_op jit(solution)/shard_map/ppermute | solution.py:413
  205.1 6.7 %all-to-all-start.3 = ((f32[8,80,128]{2,1,0:T(8,128)}), f32[8,80,128]{2,1,0:T(8,128)S(1)}, u32[]{:S(2)}, u32[]{:S(2)}) async-start(f32[8,80,128]{2,1,0:T(8,128)} %shard_map.145), calls=%async_computation.3 | async-start | bytes 655360 | tf_op jit(solution)/shard_map/all_to_all | solution.py:474
  214.2 3.2 %shard_map.144 = (bf16[128,2048]{1,0:T(8,128)(2,1)}, bf16[128,2048]{1,0:T(8,128)(2,1)}) custom-call(s32[16]{0:T(128)S(1)} %compare_select_fusion.1.place, bf16[256,4096]{1,0:T(8,128)(2,1)S(1)} %bitcast.20, bf16[128,256]{1,0:T(8,128)(2,1)} %get-tuple-element.66.spread, f32[128,64]{1,0:T(8,128)S(1)} %get-tuple-element.74.weight, ...), custom_call_target="tpu_custom_call" | custom-call | tf_op jit(solution)/shard_map/pallas_call | solution.py:64
  (88 shorter events, 58.6 us)
Async XLA Ops:
  5.5 35.9 %all-to-all-start = ((bf16[8,32,4224]{2,1,0:T(8,128)(2,1)}), bf16[8,32,4224]{2,1,0:T(8,128)(2,1)S(1)}, u32[]{:S(2)}, u32[]{:S(2)}) async-start(bf16[8,32,4224]{2,1,0:T(8,128)(2,1)} %bitcast.23), calls=%async_computation | async-start | bytes 4325376 | tf_op jit(solution)/shard_map/all_to_all | solution.py:474
  14.9 2.4 %collective-permute-start = (bf16[400,512]{1,0:T(8,128)(2,1)S(1)}, bf16[400,512]{1,0:T(8,128)(2,1)S(1)}, u32[]{:S(2)}, u32[]{:S(2)}) collective-permute-start(bf16[400,512]{1,0:T(8,128)(2,1)S(1)} %get-tuple-element.54), channel_id=1, source_target_pairs={{0,8},{8,0},{16,24},{24,16},{32,40},{40,32},{48,56},{56,48},{64,72... | collective-permute-start | bytes 1228808 | tf_op jit(solution)/shard_map/ppermute | solution.py:413
  17.9 36.8 %collective-permute-start.3 = (bf16[800,512]{1,0:T(8,128)(2,1)S(1)}, bf16[800,512]{1,0:T(8,128)(2,1)}, u32[]{:S(2)}, u32[]{:S(2)}) collective-permute-start(bf16[800,512]{1,0:T(8,128)(2,1)S(1)} %shard_map.137.refs_0_), channel_id=1, source_target_pairs={{0,64},{8,72},{16,80},{24,88},{32,96},{40,104},{48,112},{56,120},{... | collective-permute-start | bytes 2457608 | tf_op jit(solution)/shard_map/ppermute | solution.py:413
  41.3 57.5 %collective-permute-start.6 = (bf16[256,4224]{1,0:T(8,128)(2,1)S(1)}, bf16[256,4224]{1,0:T(8,128)(2,1)S(1)}, u32[]{:S(2)}, u32[]{:S(2)}) collective-permute-start(bf16[256,4224]{1,0:T(8,128)(2,1)S(1)} %bitcast.14), channel_id=1, source_target_pairs={{0,8},{8,0},{16,24},{24,16},{32,40},{40,32},{48,56},{56,48},{64,72... | collective-permute-start | bytes 6488072 | tf_op jit(solution)/shard_map/ppermute | solution.py:413
  44.6 22.4 %collective-permute-start.2 = (bf16[800,512]{1,0:T(8,128)(2,1)S(1)}, bf16[800,512]{1,0:T(8,128)(2,1)S(1)}, u32[]{:S(2)}, u32[]{:S(2)}) collective-permute-start(bf16[800,512]{1,0:T(8,128)(2,1)S(1)} %shard_map.137.refs_0_), channel_id=1, source_target_pairs={{0,16},{8,24},{16,32},{24,40},{32,48},{40,56},{48,0},{56,8},{64,80... | collective-permute-start | bytes 2457608 | tf_op jit(solution)/shard_map/ppermute | solution.py:413
  54.7 20.1 %collective-permute-start.5 = (bf16[800,512]{1,0:T(8,128)(2,1)}, bf16[800,512]{1,0:T(8,128)(2,1)S(1)}, u32[]{:S(2)}, u32[]{:S(2)}) collective-permute-start(bf16[800,512]{1,0:T(8,128)(2,1)} %collective-permute-done.3.refs_3_), channel_id=1, source_target_pairs={{0,48},{8,56},{16,0},{24,8},{32,16},{40,24},{48,32},{56,40},{64,11... | collective-permute-start | bytes 2457608 | tf_op jit(solution)/shard_map/ppermute | solution.py:413
  58.4 33.8 %collective-permute-start.1 = (bf16[800,512]{1,0:T(8,128)(2,1)S(1)}, bf16[800,512]{1,0:T(8,128)(2,1)S(1)}, u32[]{:S(2)}, u32[]{:S(2)}) collective-permute-start(bf16[800,512]{1,0:T(8,128)(2,1)S(1)} %shard_map.137.refs_0_), channel_id=1, source_target_pairs={{0,48},{8,56},{16,0},{24,8},{32,16},{40,24},{48,32},{56,40},{64,11... | collective-permute-start | bytes 2457608 | tf_op jit(solution)/shard_map/ppermute | solution.py:413
  66.9 25.3 %collective-permute-start.4 = (bf16[800,512]{1,0:T(8,128)(2,1)S(1)}, bf16[800,512]{1,0:T(8,128)(2,1)S(1)}, u32[]{:S(2)}, u32[]{:S(2)}) collective-permute-start(bf16[800,512]{1,0:T(8,128)(2,1)S(1)} %collective-permute-done.2.refs_2_), channel_id=1, source_target_pairs={{0,16},{8,24},{16,32},{24,40},{32,48},{40,56},{48,0},{56,8},{64,80... | collective-permute-start | bytes 2457608 | tf_op jit(solution)/shard_map/ppermute | solution.py:413
  67.0 38.0 %collective-permute-start.7 = (bf16[800,512]{1,0:T(8,128)(2,1)}, bf16[800,512]{1,0:T(8,128)(2,1)S(1)}, u32[]{:S(2)}, u32[]{:S(2)}) collective-permute-start(bf16[800,512]{1,0:T(8,128)(2,1)} %collective-permute-done.3.refs_3_), channel_id=1, source_target_pairs={{0,16},{8,24},{16,32},{24,40},{32,48},{40,56},{48,0},{56,8},{64,80... | collective-permute-start | bytes 2457608 | tf_op jit(solution)/shard_map/ppermute | solution.py:413
  74.8 35.0 %collective-permute-start.8 = (bf16[800,512]{1,0:T(8,128)(2,1)S(1)}, bf16[800,512]{1,0:T(8,128)(2,1)S(1)}, u32[]{:S(2)}, u32[]{:S(2)}) collective-permute-start(bf16[800,512]{1,0:T(8,128)(2,1)S(1)} %collective-permute-done.5.refs_5_), channel_id=1, source_target_pairs={{0,48},{8,56},{16,0},{24,8},{32,16},{40,24},{48,32},{56,40},{64,11... | collective-permute-start | bytes 2457608 | tf_op jit(solution)/shard_map/ppermute | solution.py:413
  117.1 12.0 %collective-permute-start.9 = (bf16[256,4096]{1,0:T(8,128)(2,1)S(1)}, bf16[256,4096]{1,0:T(8,128)(2,1)S(1)}, u32[]{:S(2)}, u32[]{:S(2)}) collective-permute-start(bf16[256,4096]{1,0:T(8,128)(2,1)S(1)} %get-tuple-element.65), channel_id=1, source_target_pairs={{0,8},{8,0},{16,24},{24,16},{32,40},{40,32},{48,56},{56,48},{64,72... | collective-permute-start | bytes 6291464 | tf_op jit(solution)/shard_map/ppermute | solution.py:413
  125.6 22.7 %collective-permute-start.14 = (bf16[768,512]{1,0:T(8,128)(2,1)}, bf16[768,512]{1,0:T(8,128)(2,1)}, u32[]{:S(2)}, u32[]{:S(2)}) collective-permute-start(bf16[768,512]{1,0:T(8,128)(2,1)} %get-tuple-element.91), channel_id=1, source_target_pairs={{0,48},{8,56},{16,0},{24,8},{32,16},{40,24},{48,32},{56,40},{64,11... | collective-permute-start | bytes 2359304 | tf_op jit(solution)/shard_map/ppermute | solution.py:413
  131.2 53.2 %all-to-all-start.1 = ((bf16[8,32,4096]{2,1,0:T(8,128)(2,1)}), bf16[8,32,4096]{2,1,0:T(8,128)(2,1)S(1)}, u32[]{:S(2)}, u32[]{:S(2)}) async-start(bf16[8,32,4096]{2,1,0:T(8,128)(2,1)} %bitcast.22), calls=%async_computation.1 | async-start | bytes 4194304 | tf_op jit(solution)/shard_map/all_to_all | solution.py:474
  138.7 19.9 %collective-permute-start.10 = (bf16[768,512]{1,0:T(8,128)(2,1)}, bf16[768,512]{1,0:T(8,128)(2,1)S(1)}, u32[]{:S(2)}, u32[]{:S(2)}) collective-permute-start(bf16[768,512]{1,0:T(8,128)(2,1)} %get-tuple-element.86), channel_id=1, source_target_pairs={{0,16},{8,24},{16,32},{24,40},{32,48},{40,56},{48,0},{56,8},{64,80... | collective-permute-start | bytes 2359304 | tf_op jit(solution)/shard_map/ppermute | solution.py:413
  145.5 30.0 %collective-permute-start.13 = (bf16[768,512]{1,0:T(8,128)(2,1)S(1)}, bf16[768,512]{1,0:T(8,128)(2,1)S(1)}, u32[]{:S(2)}, u32[]{:S(2)}) collective-permute-start(bf16[768,512]{1,0:T(8,128)(2,1)S(1)} %copy-done.19), channel_id=1, source_target_pairs={{0,16},{8,24},{16,32},{24,40},{32,48},{40,56},{48,0},{56,8},{64,80... | collective-permute-start | bytes 2359304 | tf_op jit(solution)/shard_map/ppermute | solution.py:413
  145.6 50.4 %collective-permute-start.12 = (bf16[768,512]{1,0:T(8,128)(2,1)}, bf16[768,512]{1,0:T(8,128)(2,1)}, u32[]{:S(2)}, u32[]{:S(2)}) collective-permute-start(bf16[768,512]{1,0:T(8,128)(2,1)} %get-tuple-element.87), channel_id=1, source_target_pairs={{0,48},{8,56},{16,0},{24,8},{32,16},{40,24},{48,32},{56,40},{64,11... | collective-permute-start | bytes 2359304 | tf_op jit(solution)/shard_map/ppermute | solution.py:413
  149.9 25.6 %collective-permute-start.17 = (bf16[768,256]{1,0:T(8,128)(2,1)S(1)}, bf16[768,256]{1,0:T(8,128)(2,1)S(1)}, u32[]{:S(2)}, u32[]{:S(2)}) collective-permute-start(bf16[768,256]{1,0:T(8,128)(2,1)S(1)} %get-tuple-element.97), channel_id=1, source_target_pairs={{0,48},{8,56},{16,0},{24,8},{32,16},{40,24},{48,32},{56,40},{64,11... | collective-permute-start | bytes 1179656 | tf_op jit(solution)/shard_map/ppermute | solution.py:413
  159.7 36.3 %collective-permute-start.11 = (bf16[768,512]{1,0:T(8,128)(2,1)}, bf16[768,512]{1,0:T(8,128)(2,1)}, u32[]{:S(2)}, u32[]{:S(2)}) collective-permute-start(bf16[768,512]{1,0:T(8,128)(2,1)} %add_convert_fusion.1), channel_id=1, source_target_pairs={{0,16},{8,24},{16,32},{24,40},{32,48},{40,56},{48,0},{56,8},{64,80... | collective-permute-start | bytes 2359304 | tf_op jit(solution)/shard_map/ppermute | solution.py:413
  159.7 21.7 %collective-permute-start.15 = (bf16[768,256]{1,0:T(8,128)(2,1)S(1)}, bf16[768,256]{1,0:T(8,128)(2,1)S(1)}, u32[]{:S(2)}, u32[]{:S(2)}) collective-permute-start(bf16[768,256]{1,0:T(8,128)(2,1)S(1)} %get-tuple-element.98), channel_id=1, source_target_pairs={{0,48},{8,56},{16,0},{24,8},{32,16},{40,24},{48,32},{56,40},{64,11... | collective-permute-start | bytes 1179656 | tf_op jit(solution)/shard_map/ppermute | solution.py:413
  178.6 17.4 %collective-permute-start.18 = (bf16[768,256]{1,0:T(8,128)(2,1)}, bf16[768,256]{1,0:T(8,128)(2,1)}, u32[]{:S(2)}, u32[]{:S(2)}) collective-permute-start(bf16[768,256]{1,0:T(8,128)(2,1)} %shard_map.151), channel_id=1, source_target_pairs={{0,64},{8,72},{16,80},{24,88},{32,96},{40,104},{48,112},{56,120},{... | collective-permute-start | bytes 1179656 | tf_op jit(solution)/shard_map/ppermute | solution.py:413
  184.3 11.7 %collective-permute-start.16 = (bf16[768,256]{1,0:T(8,128)(2,1)}, bf16[768,256]{1,0:T(8,128)(2,1)}, u32[]{:S(2)}, u32[]{:S(2)}) collective-permute-start(bf16[768,256]{1,0:T(8,128)(2,1)} %shard_map.150), channel_id=1, source_target_pairs={{0,64},{8,72},{16,80},{24,88},{32,96},{40,104},{48,112},{56,120},{... | collective-permute-start | bytes 1179656 | tf_op jit(solution)/shard_map/ppermute | solution.py:413
  187.9 16.4 %all-to-all-start.2 = ((bf16[16,96,128]{2,1,0:T(8,128)(2,1)}), bf16[16,96,128]{2,1,0:T(8,128)(2,1)S(1)}, u32[]{:S(2)}, u32[]{:S(2)}) async-start(bf16[16,96,128]{2,1,0:T(8,128)(2,1)} %get-tuple-element.80), calls=%async_computation.2 | async-start | bytes 786432 | tf_op jit(solution)/shard_map/all_to_all | solution.py:474
  199.5 12.2 %collective-permute-start.19 = (bf16[384,512]{1,0:T(8,128)(2,1)}, bf16[384,512]{1,0:T(8,128)(2,1)S(1)}, u32[]{:S(2)}, u32[]{:S(2)}) collective-permute-start(bf16[384,512]{1,0:T(8,128)(2,1)} %get-tuple-element.93), channel_id=1, source_target_pairs={{0,8},{8,0},{16,24},{24,16},{32,40},{40,32},{48,56},{56,48},{64,72... | collective-permute-start | bytes 1179656 | tf_op jit(solution)/shard_map/ppermute | solution.py:413
  205.1 14.6 %all-to-all-start.3 = ((f32[8,80,128]{2,1,0:T(8,128)}), f32[8,80,128]{2,1,0:T(8,128)S(1)}, u32[]{:S(2)}, u32[]{:S(2)}) async-start(f32[8,80,128]{2,1,0:T(8,128)} %shard_map.145), calls=%async_computation.3 | async-start | bytes 655360 | tf_op jit(solution)/shard_map/all_to_all | solution.py:474
  (20 other events, 179.0 us)
where the time goes:
time: 223 us; the launch traced here: 220 us
  waiting for transfers between devices  99.3 us (45%)
  starting transfers between devices  60.1 us (27%)
  Pallas kernels  44.9 us (20%)
  local copies, waits for them, and re-layouts  10.3 us (5%)
  other arithmetic  4.78 us (2%)
    ppermute x20, waiting for transfers between devices, send(): return lax.ppermute(v, DP, pairs)  72 us
    pallas_call x19, Pallas kernels, call(): pl.pallas_call(kernel, out_shape=out_shape, in_specs=specs, out_specs=[ou...  44.9 us
    ppermute x20, starting transfers between devices, send(): return lax.ppermute(v, DP, pairs)  30.4 us
    all_to_all x4, starting transfers between devices, exchange(): return lax.all_to_all(v, axis, split_axis=0, concat_axis=0, tiled=True)  29.8 us
    all_to_all x4, waiting for transfers between devices, exchange(): return lax.all_to_all(v, axis, split_axis=0, concat_axis=0, tiled=True)  27.2 us
    unnamed x41, local copies, waits for them, and re-layouts  10.3 us
    convert_element_type x3, other arithmetic, plus(): return total.astype(BF)  4.77 us
  transfers between devices with their start and end apart: 24, of which 13 were waited for; matrix products, arithmetic and copies ran while one was open for 2% of the time, Pallas kernels for 15%

commit v1 on v0

--- a/solution.py
+++ b/solution.py
@@ -19,6 +19,8 @@
 WIDE = 2 * D + 128
 ROWS = 800
 CHIPS = 8
+LEFT, RIGHT = slice(0, BK), slice(BK, HALF)
+SIDES = (LEFT, RIGHT)
 F32 = jnp.float32
 BF = jnp.bfloat16
 
@@ -171,14 +173,16 @@
 
 
 def fetch(sources, held, sems):
-    copies = [
-        pltpu.make_async_copy(source, held.at[n], sems.at[n]) for n, source in enumerate(sources)
-    ]
+    copies = []
+    for n, source in enumerate(sources):
+        for h, part in enumerate(source):
+            target = held.at[n] if len(source) == 1 else held.at[n, :, SIDES[h]]
+            copies.append(pltpu.make_async_copy(part, target, sems.at[n, h]))
     for c in copies:
         c.start()
     for c in copies:
         c.wait()
-    return [held.at[n] for n in range(len(copies))]
+    return [held.at[n] for n in range(len(sources))]
 
 
 def keep_products(rows, pieces, sums, slot_logits):
@@ -191,8 +195,8 @@
 
 
 def early_kernel(rows, *refs):
-    sums, slot_logits, routed, held, sems = refs[6:]
-    pieces = fetch(refs[:6], held, sems)
+    sums, slot_logits, routed, held, sems = refs[7:]
+    pieces = fetch([refs[n : n + 1] for n in range(5)] + [refs[5:7]], held, sems)
     keep_products(rows, pieces, sums, slot_logits)
     for n in range(6):
         for c in range(2):
@@ -204,8 +208,8 @@
 
 
 def late_kernel(place, *refs):
-    act, scaled, grad_gate, grad_up, routed, held, sems = refs[8:]
-    pieces = fetch(refs[6:8], held, sems)
+    act, scaled, grad_gate, grad_up, routed, held, sems = refs[9:]
+    pieces = fetch([refs[6:7], refs[7:9]], held, sems)
     lane = lax.broadcasted_iota(jnp.int32, (SLOTS, 64), 1)
     for i in range(2):
         rows, sums, slot_logits = refs[3 * i : 3 * i + 3]
@@ -234,16 +238,22 @@
 
 
 def output_kernel(i):
-    def kernel(rows, act, grad_gate, grad_up, first, last, out, gain):
+    def kernel(rows, act, grad_gate, grad_up, first, last, *refs):
+        out, gain = refs[-2:]
         some = slice(i * SLOTS, (i + 1) * SLOTS)
         for b in range(CHIPS):
             cols = slice(b * BK, (b + 1) * BK)
+            more = slice(D + b * BK, D + (b + 1) * BK)
             piece = first.at[EARLY.index(b)] if b in EARLY else last.at[LATE.index(b)]
-            out[:, cols] = nt(act[some, :], piece[512:768, :]).astype(BF)
+            made = nt(act[some, :], piece[512:768, :])
             total = nt(grad_gate[some, :], piece[0:256, :])
             total = total + nt(grad_up[some, :], piece[256:512, :])
-            out[:, D + b * BK : D + (b + 1) * BK] = total.astype(BF)
             gain[:, cols] = jnp.sum(total * rows[:, cols].astype(F32), axis=0, keepdims=True)
+            if len(refs) == 3:
+                made = made + refs[0][:, cols].astype(F32)
+                total = total + refs[0][:, more].astype(F32)
+            out[:, cols] = made.astype(BF)
+            out[:, more] = total.astype(BF)
 
     return kernel
 
@@ -255,17 +265,26 @@
         for n, b in enumerate(blocks):
             slot = n % 3
             if n >= 3:
-                copies[n - 3].wait()
+                for c in copies[n - 3]:
+                    c.wait()
             x = flipped[b * BK : (b + 1) * BK, :]
             stage[slot, 0:256, :] = nn(x, grad_gate[...]).astype(BF)
             stage[slot, 256:512, :] = nn(x, grad_up[...]).astype(BF)
             stage[slot, 512:768, :] = nn(
                 flipped[D + b * BK : D + (b + 1) * BK, :], scaled[...]
             ).astype(BF)
-            copies[n] = pltpu.make_async_copy(stage.at[slot], outs[n], sems.at[slot])
-            copies[n].start()
+            if b == 3:
+                copies[n] = [
+                    pltpu.make_async_copy(stage.at[slot, :, side], out, sems.at[slot, h])
+                    for h, (side, out) in enumerate(zip(SIDES, (outs[n], outs[-1])))
+                ]
+            else:
+                copies[n] = [pltpu.make_async_copy(stage.at[slot], outs[n], sems.at[slot, 0])]
+            for c in copies[n]:
+                c.start()
         for n in range(max(0, len(blocks) - 3), len(blocks)):
-            copies[n].wait()
+            for c in copies[n]:
+                c.wait()
 
     return kernel
 
@@ -353,15 +372,16 @@
         ).astype(BF)
 
 
-def total_kernel(place, here, ahead, behind, left, right, give, keep):
+def total_kernel(place, here, *refs):
+    halves, give, keep = refs[:6], refs[6], refs[7]
     core = place[8]
     for m in range(3):
         for out, side in ((give, 1 - core), (keep, core)):
             rows = at(m * BK + side * TOK, TOK)
-            for h, last in enumerate((left, right)):
-                cols = slice(h * BK, (h + 1) * BK)
-                total = here[rows, cols].astype(F32) + ahead[rows, cols].astype(F32)
-                total = total + behind[rows, cols].astype(F32) + last[rows, :].astype(F32)
+            for h, cols in enumerate(SIDES):
+                total = here[rows, cols].astype(F32)
+                for v in halves[h::2]:
+                    total = total + v[rows, :].astype(F32)
                 out[m * TOK : (m + 1) * TOK, cols] = total.astype(BF)
 
 
@@ -415,13 +435,13 @@
 
 def gather_pieces(own):
     across = send(own, ACROSS)
+    own_3 = send(own, AHEAD)
     own_1 = send(own, BEHIND)
-    own_3 = send(own, AHEAD)
-    across_1 = send(across, BEHIND)
+    own_2 = send(own_3, AHEAD)
+    across_1 = [send(across[:, side], BEHIND) for side in SIDES]
     across_3 = send(across, AHEAD)
-    own_2 = send(own_3, AHEAD)
-    across_2 = send(across_1, BEHIND)
-    return (own, own_1, own_2, own_3, across, across_1, across_2, across_3)
+    across_2 = [send(v, BEHIND) for v in across_1]
+    return ([own], [own_1], [own_2], [own_3], [across], across_1, across_2, [across_3])
 
 
 def plus(*values):
@@ -432,15 +452,20 @@
 
 
 def reduce_pieces(parts):
-    cols = [slice(h * BK, (h + 1) * BK) for h in range(2)]
     across_2 = send(parts[6], BEHIND)
+    across_1 = send(parts[5], AHEAD)
     own_2 = send(parts[2], AHEAD)
-    across_1 = send(parts[5], AHEAD)
-    across_3 = [send(plus(parts[7][:, cols[h]], across_2[:, cols[h]]), BEHIND) for h in range(2)]
-    own_3 = send(parts[3], BEHIND)
-    own_1 = send(plus(parts[1], own_2), AHEAD)
-    across = [send(plus_half(h, parts[4], across_1, across_3[h]), ACROSS) for h in range(2)]
-    return parts[0], own_1, own_3, *across
+    across_3 = [send(plus(parts[7][:, side], across_2[:, side]), BEHIND) for side in SIDES]
+    own_3 = [send(v, BEHIND) for v in (parts[3], parts[8])]
+    own_1 = [send(plus(parts[1][:, side], own_2[:, side]), AHEAD) for side in SIDES]
+    across = [
+        send(v, ACROSS)
+        for v in (
+            plus(parts[4][:, LEFT], across_1[:, LEFT], across_3[0]),
+            plus_half(1, parts[4], across_1, across_3[1]),
+        )
+    ]
+    return parts[0], *own_1, *own_3, *across
 
 
 def sum_kernel(h):
@@ -488,7 +513,7 @@
     weights = (gate_weight[0], up_weight[0], down_weight[0])
     away, keep_own = call(
         pack_kernel, [sds((400, HALF), BF)] * 2, place, *weights, router_weight.T, smem=1,
-        limit=MiB(2), far=(1, 2, 3), scratch=[pltpu.SemaphoreType.DMA((2, 3))],
+        limit=MiB(2), far=(1, 2, 3), dram=(4,), scratch=[pltpu.SemaphoreType.DMA((2, 3))],
     )
     other = send(away, SIBLING)
     hidden, xs, gains, root, spread, chosen, sent = call(
@@ -509,8 +534,8 @@
     sums, slot_logits, routed_early, held_early = call(
         early_kernel,
         shapes + [pltpu.HBM((64, 6 * BK), BF), pltpu.VMEM((6, ROWS, HALF), BF)],
-        rows, *[pieces[b] for b in EARLY], limit=MiB(6), far=range(1, 7),
-        scratch=[pltpu.SemaphoreType.DMA((6,))],
+        rows, *[v for b in EARLY for v in pieces[b]], limit=MiB(6), far=range(1, 8),
+        scratch=[pltpu.SemaphoreType.DMA((6, 2))],
     )
     sums_other, logits_other = call(
         early_other_kernel, shapes, rows_other, held_early, limit=MiB(6),
@@ -520,27 +545,27 @@
         [sds((2 * SLOTS, HALF), BF)] * 4
         + [pltpu.HBM((64, 2 * BK), BF), pltpu.VMEM((2, ROWS, HALF), BF)],
         place, rows, sums, slot_logits, rows_other, sums_other, logits_other,
-        *[pieces[b] for b in LATE], smem=1, limit=MiB(8), far=(7, 8),
-        scratch=[pltpu.SemaphoreType.DMA((2,))],
-    )
-    (partial_other, gain_other), (partial, gain_mine) = (
-        call(
-            output_kernel(i), [sds((SLOTS, 2 * D), BF), sds((1, D), F32)],
-            source, act, grad_gate, grad_up, held_early, held_late, limit=MiB(6),
-        )
-        for i, source in ((1, rows_other), (0, rows))
-    )
-    output = plus(partial, send(partial_other, SIBLING))
+        *[v for b in LATE for v in pieces[b]], smem=1, limit=MiB(8), far=(7, 8, 9),
+        scratch=[pltpu.SemaphoreType.DMA((2, 2))],
+    )
+    shapes = [sds((SLOTS, 2 * D), BF), sds((1, D), F32)]
+    operands = (act, grad_gate, grad_up, held_early, held_late)
+    partial, gain_other = call(output_kernel(1), shapes, rows_other, *operands, limit=MiB(6))
+    received = send(partial, SIBLING)
+    output, gain_mine = call(output_kernel(0), shapes, rows, *operands, received, limit=MiB(8))
     returned = exchange(output.reshape(WIN, CAP, 2 * D), "expert")
     returned = returned.reshape(SLOTS, 2 * D)
     parts = {}
-    for blocks in ((6, 2, 5), (7, 3, 1, 4, 0)):
+    for blocks in ((6, 5, 2), (3, 7, 1, 4, 0)):
+        shapes = [pltpu.HBM((768, BK if b == 3 else HALF), BF) for b in blocks]
+        if 3 in blocks:
+            shapes.append(pltpu.HBM((768, BK), BF))
         made = call(
-            grads_kernel(blocks), [pltpu.HBM((768, HALF), BF)] * len(blocks),
-            flipped, scaled, grad_gate, grad_up, limit=MiB(5), far_out=True,
-            scratch=[pltpu.VMEM((3, 768, HALF), BF), pltpu.SemaphoreType.DMA((3,))],
+            grads_kernel(blocks), shapes, flipped, scaled, grad_gate, grad_up,
+            limit=MiB(5), far_out=True,
+            scratch=[pltpu.VMEM((3, 768, HALF), BF), pltpu.SemaphoreType.DMA((3, 2))],
         )
-        parts.update(zip(blocks, made))
+        parts.update(zip(blocks + (8,), made))
     give, keep = call(
         total_kernel, [sds((384, HALF), BF)] * 2, place, *reduce_pieces(parts),
         smem=1, limit=MiB(6),

time: 223 us -> 216 us (0.969)
  starting transfers between devices: 60.1 us -> 54.6 us
    all_to_all x4, starting transfers between devices: 29.8 us -> 21.9 us  [exchange(): return lax.all_to_all(v, axis, split_axis=0, concat_axis=0, tiled=True)]
    ppermute x20 -> x24, starting transfers between devices: 30.4 us -> 32.7 us  [send(): return lax.ppermute(v, DP, pairs)]
    pallas_call x19 -> x18, Pallas kernels: 44.9 us -> 42.8 us  [call(): pl.pallas_call(kernel, out_shape=out_shape, in_specs=specs, out_specs=[ou...]
    unnamed x41 -> x51, local copies, waits for them, and re-layouts: 10.3 us -> 11.4 us
    ppermute x20 -> x24, waiting for transfers between devices: 72 us -> 72.9 us  [send(): return lax.ppermute(v, DP, pairs)]
  transfers between devices with their start and end apart: 24 -> 28, of which waited for: 13 -> 11; matrix products, arithmetic and copies ran while one was open for 2% -> 2% of each run, Pallas kernels for 15% -> 15%
where the time goes in v1:
time: 216 us; the launch traced here: 214 us
  waiting for transfers between devices  100 us (46%)
  starting transfers between devices  54.6 us (25%)
  Pallas kernels  42.8 us (20%)
  local copies, waits for them, and re-layouts  11.5 us (5%)
  other arithmetic  3.72 us (2%)
    ppermute x24, waiting for transfers between devices, send(): return lax.ppermute(v, DP, pairs)  72.9 us
    pallas_call x18, Pallas kernels, call(): pl.pallas_call(kernel, out_shape=out_shape, in_specs=specs, out_specs=[ou...  42.8 us
    ppermute x24, starting transfers between devices, send(): return lax.ppermute(v, DP, pairs)  32.7 us
    all_to_all x4, waiting for transfers between devices, exchange(): return lax.all_to_all(v, axis, split_axis=0, concat_axis=0, tiled=True)  27.5 us
    all_to_all x4, starting transfers between devices, exchange(): return lax.all_to_all(v, axis, split_axis=0, concat_axis=0, tiled=True)  21.9 us
    unnamed x51, local copies, waits for them, and re-layouts  11.4 us
  transfers between devices with their start and end apart: 28, of which 11 were waited for; matrix products, arithmetic and copies ran while one was open for 2% of the time, Pallas kernels for 15%

profile of v1, /device:TPU:1, one launch (start us, length us, event | category | flops | bytes accessed | tf_op | source)
XLA Modules:
  0.0 214.0 jit_solution(11992400520075851872)
XLA Ops:
  1.4 4.0 %shard_map.135 = (bf16[128,2048]{1,0:T(8,128)(2,1)}, bf16[128,2048]{1,0:T(8,128)(2,1)}, f32[1,2048]{1,0:T(1,128)}, f32[128,128]{1,0:T(8,128)}, bf16[128,256]{1,0...) custom-call(s32[16]{0:T(128)S(1)} %compare_select_fusion.1.place, bf16[128,2048]{1,0:T(8,128)(2,1)} %tokens.1, ...), custom_call_target="tpu_custom_call" | custom-call | tf_op jit(solution)/shard_map/pallas_call | solution.py:66
  5.4 7.5 %all-to-all-start = ((bf16[8,32,4224]{2,1,0:T(8,128)(2,1)}), bf16[8,32,4224]{2,1,0:T(8,128)(2,1)S(1)}, u32[]{:S(2)}, u32[]{:S(2)}) async-start(bf16[8,32,4224]{2,1,0:T(8,128)(2,1)} %bitcast.22), calls=%async_computation | async-start | bytes 4325376 | tf_op jit(solution)/shard_map/all_to_all | solution.py:499
  15.9 25.3 %all-to-all-done = bf16[8,32,4224]{2,1,0:T(8,128)(2,1)S(1)} async-done(((bf16[8,32,4224]{2,1,0:T(8,128)(2,1)}), bf16[8,32,4224]{2,1,0:T(8,128)(2,1)S(1)}, u32[]{:S(2)}, u32[]{:S(2)}) %all-to-all-start) | async-done | bytes 2162720 | tf_op jit(solution)/shard_map/all_to_all | solution.py:499
  47.9 18.2 %collective-permute-done.2.refs_2_ = bf16[800,512]{1,0:T(8,128)(2,1)S(1)} collective-permute-done((bf16[800,512]{1,0:T(8,128)(2,1)S(1)}, bf16[800,512]{1,0:T(8,128)(2,1)S(1)}, u32[]{:S(2)}, u32[]{:S(2)}) %collective-permute-start.2) | collective-permute-done | bytes 819232 | tf_op jit(solution)/shard_map/ppermute | solution.py:433
  71.6 5.3 %collective-permute-done.5.refs_5_ = bf16[800,256]{1,0:T(8,128)(2,1)S(1)} collective-permute-done((bf16[800,256]{1,0:T(8,128)(2,1)S(1)}, bf16[800,256]{1,0:T(8,128)(2,1)S(1)}, u32[]{:S(2)}, u32[]{:S(2)}) %collective-permute-start.5) | collective-permute-done | bytes 409632 | tf_op jit(solution)/shard_map/ppermute | solution.py:433
  76.9 3.4 %collective-permute-start.9 = (bf16[800,256]{1,0:T(8,128)(2,1)S(1)}, bf16[800,256]{1,0:T(8,128)(2,1)S(1)}, u32[]{:S(2)}, u32[]{:S(2)}) collective-permute-start(bf16[800,256]{1,0:T(8,128)(2,1)S(1)} %collective-permute-done.5.refs_5_), channel_id=1, source_target_pairs={{0,48},{8,56},{16,0},{24,8},{32,16},{40,24},{48,32},{56,40},{64,11... | collective-permute-start | bytes 1228808 | tf_op jit(solution)/shard_map/ppermute | solution.py:433
  80.3 5.4 %collective-permute-done.6.refs_6_ = bf16[800,256]{1,0:T(8,128)(2,1)S(1)} collective-permute-done((bf16[800,256]{1,0:T(8,128)(2,1)S(1)}, bf16[800,256]{1,0:T(8,128)(2,1)S(1)}, u32[]{:S(2)}, u32[]{:S(2)}) %collective-permute-start.6) | collective-permute-done | bytes 409632 | tf_op jit(solution)/shard_map/ppermute | solution.py:433
  85.7 3.4 %collective-permute-start.10 = (bf16[800,256]{1,0:T(8,128)(2,1)S(1)}, bf16[800,256]{1,0:T(8,128)(2,1)S(1)}, u32[]{:S(2)}, u32[]{:S(2)}) collective-permute-start(bf16[800,256]{1,0:T(8,128)(2,1)S(1)} %collective-permute-done.6.refs_6_), channel_id=1, source_target_pairs={{0,48},{8,56},{16,0},{24,8},{32,16},{40,24},{48,32},{56,40},{64,11... | collective-permute-start | bytes 1228808 | tf_op jit(solution)/shard_map/ppermute | solution.py:433
  90.0 4.7 %shard_map.138 = (f32[256,1536]{1,0:T(8,128)S(1)}, f32[256,64]{1,0:T(8,128)S(1)}, bf16[64,1536]{1,0:T(8,128)(2,1)}, bf16[6,800,512]{2,1,0:T(8,128)(2,1)S(1)}) custom-call(bf16[256,4224]{1,0:T(8,128)(2,1)S(1)} %bitcast.15, bf16[800,512]{1,0:T(8,128)(2,1)} %copy-done.2, bf16[800,512]{1,0:T(8,128)(2,1)} %copy-done.16, bf16[800,512]{1,0:T(8,128)(2,1)} %copy-done.14, ...), custom_call_target="tpu_custom_call" | custom-call | tf_op jit(solution)/shard_map/pallas_call | solution.py:66
  96.3 7.8 %collective-permute-done.8.refs_6_ = bf16[800,512]{1,0:T(8,128)(2,1)S(1)} collective-permute-done((bf16[800,512]{1,0:T(8,128)(2,1)S(1)}, bf16[800,512]{1,0:T(8,128)(2,1)S(1)}, u32[]{:S(2)}, u32[]{:S(2)}) %collective-permute-start.8) | collective-permute-done | bytes 819232 | tf_op jit(solution)/shard_map/ppermute | solution.py:433
  105.3 4.4 %shard_map.140 = (bf16[512,512]{1,0:T(8,128)(2,1)S(1)}, bf16[512,512]{1,0:T(8,128)(2,1)S(1)}, bf16[512,512]{1,0:T(8,128)(2,1)S(1)}, bf16[512,512]{1,0:T(8,128)(2...) custom-call(s32[16]{0:T(128)S(1)} %compare_select_fusion.1.place, bf16[256,4224]{1,0:T(8,128)(2,1)S(1)} %bitcast.16, ...), custom_call_target="tpu_custom_call" | custom-call | tf_op jit(solution)/shard_map/pallas_call | solution.py:66
  114.4 2.8 %shard_map.149 = (bf16[768,512]{1,0:T(8,128)(2,1)}, bf16[768,512]{1,0:T(8,128)(2,1)}, bf16[768,512]{1,0:T(8,128)(2,1)}) custom-call(bf16[4096,512]{1,0:T(8,128)(2,1)S(1)} %shard_map.147.flipped, bf16[512,512]{1,0:T(8,128)(2,1)S(1)} %get-tuple-element.84.scaled, bf16[512,512]{1,0:T(8,128)(2,1)S(1)} %get-tuple-element.62.grad_gate, ...), custom_call_target="tpu_custom_call" | custom-call | tf_op jit(solution)/shard_map/pallas_call | solution.py:66
  123.0 3.6 %all-to-all-start.1 = ((bf16[8,32,4096]{2,1,0:T(8,128)(2,1)}), bf16[8,32,4096]{2,1,0:T(8,128)(2,1)S(1)}, u32[]{:S(2)}, u32[]{:S(2)}) async-start(bf16[8,32,4096]{2,1,0:T(8,128)(2,1)} %bitcast.21), calls=%async_computation.1 | async-start | bytes 4194304 | tf_op jit(solution)/shard_map/all_to_all | solution.py:499
  130.0 3.6 %shard_map.148 = (bf16[768,256]{1,0:T(8,128)(2,1)}, bf16[768,512]{1,0:T(8,128)(2,1)}, bf16[768,512]{1,0:T(8,128)(2,1)}, bf16[768,512]{1,0:T(8,128)(2,1)}, bf16[7...) custom-call(bf16[4096,512]{1,0:T(8,128)(2,1)S(1)} %copy-done.1, bf16[512,512]{1,0:T(8,128)(2,1)S(1)} %copy-done.5, ...), custom_call_target="tpu_custom_call" | custom-call | tf_op jit(solution)/shard_map/pallas_call | solution.py:66
  133.6 3.4 %collective-permute-done.18 = bf16[768,512]{1,0:T(8,128)(2,1)} collective-permute-done((bf16[768,512]{1,0:T(8,128)(2,1)}, bf16[768,512]{1,0:T(8,128)(2,1)}, u32[]{:S(2)}, u32[]{:S(2)}) %collective-permute-start.18) | collective-permute-done | bytes 786464 | tf_op jit(solution)/shard_map/ppermute | solution.py:433
  138.6 3.5 %collective-permute-start.19 = (bf16[768,256]{1,0:T(8,128)(2,1)S(1)}, bf16[768,256]{1,0:T(8,128)(2,1)S(1)}, u32[]{:S(2)}, u32[]{:S(2)}) collective-permute-start(bf16[768,256]{1,0:T(8,128)(2,1)S(1)} %get-tuple-element.100), channel_id=1, source_target_pairs={{0,48},{8,56},{16,0},{24,8},{32,16},{40,24},{48,32},{56,40},{64,11... | collective-permute-start | bytes 1179656 | tf_op jit(solution)/shard_map/ppermute | solution.py:433
  142.2 4.7 %collective-permute-done.12 = bf16[768,512]{1,0:T(8,128)(2,1)S(1)} collective-permute-done((bf16[768,512]{1,0:T(8,128)(2,1)}, bf16[768,512]{1,0:T(8,128)(2,1)S(1)}, u32[]{:S(2)}, u32[]{:S(2)}) %collective-permute-start.12) | collective-permute-done | bytes 786464 | tf_op jit(solution)/shard_map/ppermute | solution.py:433
  148.1 15.7 %collective-permute-done.17.refs_1_ = bf16[768,512]{1,0:T(8,128)(2,1)S(1)} collective-permute-done((bf16[768,512]{1,0:T(8,128)(2,1)}, bf16[768,512]{1,0:T(8,128)(2,1)S(1)}, u32[]{:S(2)}, u32[]{:S(2)}) %collective-permute-start.17) | collective-permute-done | bytes 786464 | tf_op jit(solution)/shard_map/ppermute | solution.py:433
  164.8 10.2 %collective-permute-done.21.refs_2_ = bf16[768,256]{1,0:T(8,128)(2,1)S(1)} collective-permute-done((bf16[768,256]{1,0:T(8,128)(2,1)S(1)}, bf16[768,256]{1,0:T(8,128)(2,1)S(1)}, u32[]{:S(2)}, u32[]{:S(2)}) %collective-permute-start.21) | collective-permute-done | bytes 393248 | tf_op jit(solution)/shard_map/ppermute | solution.py:433
  179.4 3.5 %shard_map.143 = (f32[128,64]{1,0:T(8,128)S(1)}, f32[128,64]{1,0:T(8,128)S(1)}, bf16[16,96,128]{2,1,0:T(8,128)(2,1)}) custom-call(s32[16]{0:T(128)S(1)} %compare_select_fusion.1.place, bf16[256,4096]{1,0:T(8,128)(2,1)S(1)} %bitcast.19, bf16[128,2048]{1,0:T(8,128)(2,1)} %cotangent.3, bf16[128,256]{1,0:T(8,128)(2,1)} %get-tuple-element.67.spread, ...), custom_call_target="tpu_custom_call" | custom-call | tf_op jit(solution)/shard_map/pallas_call | solution.py:66
  182.8 7.4 %all-to-all-start.2 = ((bf16[16,96,128]{2,1,0:T(8,128)(2,1)}), bf16[16,96,128]{2,1,0:T(8,128)(2,1)S(1)}, u32[]{:S(2)}, u32[]{:S(2)}) async-start(bf16[16,96,128]{2,1,0:T(8,128)(2,1)} %get-tuple-element.81), calls=%async_computation.2 | async-start | bytes 786432 | tf_op jit(solution)/shard_map/all_to_all | solution.py:499
  197.0 4.2 %collective-permute-start.23 = (bf16[384,512]{1,0:T(8,128)(2,1)}, bf16[384,512]{1,0:T(8,128)(2,1)S(1)}, u32[]{:S(2)}, u32[]{:S(2)}) collective-permute-start(bf16[384,512]{1,0:T(8,128)(2,1)} %get-tuple-element.95), channel_id=1, source_target_pairs={{0,8},{8,0},{16,24},{24,16},{32,40},{40,32},{48,56},{56,48},{64,72... | collective-permute-start | bytes 1179656 | tf_op jit(solution)/shard_map/ppermute | solution.py:433
  202.0 3.4 %all-to-all-start.3 = ((f32[8,80,128]{2,1,0:T(8,128)}), f32[8,80,128]{2,1,0:T(8,128)S(1)}, u32[]{:S(2)}, u32[]{:S(2)}) async-start(f32[8,80,128]{2,1,0:T(8,128)} %shard_map.145), calls=%async_computation.3 | async-start | bytes 655360 | tf_op jit(solution)/shard_map/all_to_all | solution.py:499
  207.9 3.2 %shard_map.144 = (bf16[128,2048]{1,0:T(8,128)(2,1)}, bf16[128,2048]{1,0:T(8,128)(2,1)}) custom-call(s32[16]{0:T(128)S(1)} %compare_select_fusion.1.place, bf16[256,4096]{1,0:T(8,128)(2,1)S(1)} %bitcast.20, bf16[128,256]{1,0:T(8,128)(2,1)} %get-tuple-element.67.spread, f32[128,64]{1,0:T(8,128)S(1)} %get-tuple-element.75.weight, ...), custom_call_target="tpu_custom_call" | custom-call | tf_op jit(solution)/shard_map/pallas_call | solution.py:66
  (106 shorter events, 54.5 us)
Async XLA Ops:
  5.4 35.8 %all-to-all-start = ((bf16[8,32,4224]{2,1,0:T(8,128)(2,1)}), bf16[8,32,4224]{2,1,0:T(8,128)(2,1)S(1)}, u32[]{:S(2)}, u32[]{:S(2)}) async-start(bf16[8,32,4224]{2,1,0:T(8,128)(2,1)} %bitcast.22), calls=%async_computation | async-start | bytes 4325376 | tf_op jit(solution)/shard_map/all_to_all | solution.py:499
  14.9 28.1 %collective-permute-start = (bf16[400,512]{1,0:T(8,128)(2,1)S(1)}, bf16[400,512]{1,0:T(8,128)(2,1)S(1)}, u32[]{:S(2)}, u32[]{:S(2)}) collective-permute-start(bf16[400,512]{1,0:T(8,128)(2,1)S(1)} %get-tuple-element.55), channel_id=1, source_target_pairs={{0,8},{8,0},{16,24},{24,16},{32,40},{40,32},{48,56},{56,48},{64,72... | collective-permute-start | bytes 1228808 | tf_op jit(solution)/shard_map/ppermute | solution.py:433
  41.2 53.5 %collective-permute-start.7 = (bf16[256,4224]{1,0:T(8,128)(2,1)S(1)}, bf16[256,4224]{1,0:T(8,128)(2,1)S(1)}, u32[]{:S(2)}, u32[]{:S(2)}) collective-permute-start(bf16[256,4224]{1,0:T(8,128)(2,1)S(1)} %bitcast.14), channel_id=1, source_target_pairs={{0,8},{8,0},{16,24},{24,16},{32,40},{40,32},{48,56},{56,48},{64,72... | collective-permute-start | bytes 6488072 | tf_op jit(solution)/shard_map/ppermute | solution.py:433
  43.7 22.4 %collective-permute-start.2 = (bf16[800,512]{1,0:T(8,128)(2,1)S(1)}, bf16[800,512]{1,0:T(8,128)(2,1)S(1)}, u32[]{:S(2)}, u32[]{:S(2)}) collective-permute-start(bf16[800,512]{1,0:T(8,128)(2,1)S(1)} %shard_map.137.refs_0_), channel_id=1, source_target_pairs={{0,16},{8,24},{16,32},{24,40},{32,48},{40,56},{48,0},{56,8},{64,80... | collective-permute-start | bytes 2457608 | tf_op jit(solution)/shard_map/ppermute | solution.py:433
  45.4 20.7 %collective-permute-start.3 = (bf16[800,512]{1,0:T(8,128)(2,1)S(1)}, bf16[800,512]{1,0:T(8,128)(2,1)S(1)}, u32[]{:S(2)}, u32[]{:S(2)}) collective-permute-start(bf16[800,512]{1,0:T(8,128)(2,1)S(1)} %shard_map.137.refs_0_), channel_id=1, source_target_pairs={{0,64},{8,72},{16,80},{24,88},{32,96},{40,104},{48,112},{56,120},{... | collective-permute-start | bytes 2457608 | tf_op jit(solution)/shard_map/ppermute | solution.py:433
  45.7 23.2 %collective-permute-start.1 = (bf16[800,512]{1,0:T(8,128)(2,1)S(1)}, bf16[800,512]{1,0:T(8,128)(2,1)S(1)}, u32[]{:S(2)}, u32[]{:S(2)}) collective-permute-start(bf16[800,512]{1,0:T(8,128)(2,1)S(1)} %shard_map.137.refs_0_), channel_id=1, source_target_pairs={{0,48},{8,56},{16,0},{24,8},{32,16},{40,24},{48,32},{56,40},{64,11... | collective-permute-start | bytes 2457608 | tf_op jit(solution)/shard_map/ppermute | solution.py:433
  66.1 23.0 %collective-permute-start.4 = (bf16[800,512]{1,0:T(8,128)(2,1)S(1)}, bf16[800,512]{1,0:T(8,128)(2,1)S(1)}, u32[]{:S(2)}, u32[]{:S(2)}) collective-permute-start(bf16[800,512]{1,0:T(8,128)(2,1)S(1)} %collective-permute-done.2.refs_2_), channel_id=1, source_target_pairs={{0,16},{8,24},{16,32},{24,40},{32,48},{40,56},{48,0},{56,8},{64,80... | collective-permute-start | bytes 2457608 | tf_op jit(solution)/shard_map/ppermute | solution.py:433
  68.9 35.2 %collective-permute-start.8 = (bf16[800,512]{1,0:T(8,128)(2,1)S(1)}, bf16[800,512]{1,0:T(8,128)(2,1)S(1)}, u32[]{:S(2)}, u32[]{:S(2)}) collective-permute-start(bf16[800,512]{1,0:T(8,128)(2,1)S(1)} %collective-permute-done.3.refs_3_), channel_id=1, source_target_pairs={{0,16},{8,24},{16,32},{24,40},{32,48},{40,56},{48,0},{56,8},{64,80... | collective-permute-start | bytes 2457608 | tf_op jit(solution)/shard_map/ppermute | solution.py:433
  68.9 16.7 %collective-permute-start.6 = (bf16[800,256]{1,0:T(8,128)(2,1)S(1)}, bf16[800,256]{1,0:T(8,128)(2,1)S(1)}, u32[]{:S(2)}, u32[]{:S(2)}) collective-permute-start(bf16[800,256]{1,0:T(8,128)(2,1)S(1)} %get-tuple-element.103), channel_id=1, source_target_pairs={{0,48},{8,56},{16,0},{24,8},{32,16},{40,24},{48,32},{56,40},{64,11... | collective-permute-start | bytes 1228808 | tf_op jit(solution)/shard_map/ppermute | solution.py:433
  76.9 27.2 %collective-permute-start.9 = (bf16[800,256]{1,0:T(8,128)(2,1)S(1)}, bf16[800,256]{1,0:T(8,128)(2,1)S(1)}, u32[]{:S(2)}, u32[]{:S(2)}) collective-permute-start(bf16[800,256]{1,0:T(8,128)(2,1)S(1)} %collective-permute-done.5.refs_5_), channel_id=1, source_target_pairs={{0,48},{8,56},{16,0},{24,8},{32,16},{40,24},{48,32},{56,40},{64,11... | collective-permute-start | bytes 1228808 | tf_op jit(solution)/shard_map/ppermute | solution.py:433
  85.7 18.4 %collective-permute-start.10 = (bf16[800,256]{1,0:T(8,128)(2,1)S(1)}, bf16[800,256]{1,0:T(8,128)(2,1)S(1)}, u32[]{:S(2)}, u32[]{:S(2)}) collective-permute-start(bf16[800,256]{1,0:T(8,128)(2,1)S(1)} %collective-permute-done.6.refs_6_), channel_id=1, source_target_pairs={{0,48},{8,56},{16,0},{24,8},{32,16},{40,24},{48,32},{56,40},{64,11... | collective-permute-start | bytes 1228808 | tf_op jit(solution)/shard_map/ppermute | solution.py:433
  117.3 19.7 %collective-permute-start.18 = (bf16[768,512]{1,0:T(8,128)(2,1)}, bf16[768,512]{1,0:T(8,128)(2,1)}, u32[]{:S(2)}, u32[]{:S(2)}) collective-permute-start(bf16[768,512]{1,0:T(8,128)(2,1)} %get-tuple-element.93), channel_id=1, source_target_pairs={{0,48},{8,56},{16,0},{24,8},{32,16},{40,24},{48,32},{56,40},{64,11... | collective-permute-start | bytes 2359304 | tf_op jit(solution)/shard_map/ppermute | solution.py:433
  123.0 56.4 %all-to-all-start.1 = ((bf16[8,32,4096]{2,1,0:T(8,128)(2,1)}), bf16[8,32,4096]{2,1,0:T(8,128)(2,1)S(1)}, u32[]{:S(2)}, u32[]{:S(2)}) async-start(bf16[8,32,4096]{2,1,0:T(8,128)(2,1)} %bitcast.21), calls=%async_computation.1 | async-start | bytes 4194304 | tf_op jit(solution)/shard_map/all_to_all | solution.py:499
  126.6 20.3 %collective-permute-start.12 = (bf16[768,512]{1,0:T(8,128)(2,1)}, bf16[768,512]{1,0:T(8,128)(2,1)S(1)}, u32[]{:S(2)}, u32[]{:S(2)}) collective-permute-start(bf16[768,512]{1,0:T(8,128)(2,1)} %get-tuple-element.87), channel_id=1, source_target_pairs={{0,16},{8,24},{16,32},{24,40},{32,48},{40,56},{48,0},{56,8},{64,80... | collective-permute-start | bytes 2359304 | tf_op jit(solution)/shard_map/ppermute | solution.py:433
  126.7 37.1 %collective-permute-start.17 = (bf16[768,512]{1,0:T(8,128)(2,1)}, bf16[768,512]{1,0:T(8,128)(2,1)S(1)}, u32[]{:S(2)}, u32[]{:S(2)}) collective-permute-start(bf16[768,512]{1,0:T(8,128)(2,1)} %get-tuple-element.91), channel_id=1, source_target_pairs={{0,16},{8,24},{16,32},{24,40},{32,48},{40,56},{48,0},{56,8},{64,80... | collective-permute-start | bytes 2359304 | tf_op jit(solution)/shard_map/ppermute | solution.py:433
  138.6 25.2 %collective-permute-start.19 = (bf16[768,256]{1,0:T(8,128)(2,1)S(1)}, bf16[768,256]{1,0:T(8,128)(2,1)S(1)}, u32[]{:S(2)}, u32[]{:S(2)}) collective-permute-start(bf16[768,256]{1,0:T(8,128)(2,1)S(1)} %get-tuple-element.100), channel_id=1, source_target_pairs={{0,48},{8,56},{16,0},{24,8},{32,16},{40,24},{48,32},{56,40},{64,11... | collective-permute-start | bytes 1179656 | tf_op jit(solution)/shard_map/ppermute | solution.py:433
  142.1 35.8 %collective-permute-start.15 = (bf16[768,256]{1,0:T(8,128)(2,1)S(1)}, bf16[768,256]{1,0:T(8,128)(2,1)S(1)}, u32[]{:S(2)}, u32[]{:S(2)}) collective-permute-start(bf16[768,256]{1,0:T(8,128)(2,1)S(1)} %copy-done.24), channel_id=1, source_target_pairs={{0,48},{8,56},{16,0},{24,8},{32,16},{40,24},{48,32},{56,40},{64,11... | collective-permute-start | bytes 1179656 | tf_op jit(solution)/shard_map/ppermute | solution.py:433
  142.2 48.1 %collective-permute-start.16 = (bf16[768,256]{1,0:T(8,128)(2,1)}, bf16[768,256]{1,0:T(8,128)(2,1)}, u32[]{:S(2)}, u32[]{:S(2)}) collective-permute-start(bf16[768,256]{1,0:T(8,128)(2,1)} %get-tuple-element.89), channel_id=1, source_target_pairs={{0,48},{8,56},{16,0},{24,8},{32,16},{40,24},{48,32},{56,40},{64,11... | collective-permute-start | bytes 1179656 | tf_op jit(solution)/shard_map/ppermute | solution.py:433
  146.9 28.1 %collective-permute-start.21 = (bf16[768,256]{1,0:T(8,128)(2,1)S(1)}, bf16[768,256]{1,0:T(8,128)(2,1)S(1)}, u32[]{:S(2)}, u32[]{:S(2)}) collective-permute-start(bf16[768,256]{1,0:T(8,128)(2,1)S(1)} %get-tuple-element.99), channel_id=1, source_target_pairs={{0,48},{8,56},{16,0},{24,8},{32,16},{40,24},{48,32},{56,40},{64,11... | collective-permute-start | bytes 1179656 | tf_op jit(solution)/shard_map/ppermute | solution.py:433
  163.8 26.5 %collective-permute-start.13 = (bf16[768,256]{1,0:T(8,128)(2,1)}, bf16[768,256]{1,0:T(8,128)(2,1)}, u32[]{:S(2)}, u32[]{:S(2)}) collective-permute-start(bf16[768,256]{1,0:T(8,128)(2,1)} %get-tuple-element.102), channel_id=1, source_target_pairs={{0,16},{8,24},{16,32},{24,40},{32,48},{40,56},{48,0},{56,8},{64,80... | collective-permute-start | bytes 1179656 | tf_op jit(solution)/shard_map/ppermute | solution.py:433
  163.8 26.5 %collective-permute-start.14 = (bf16[768,256]{1,0:T(8,128)(2,1)}, bf16[768,256]{1,0:T(8,128)(2,1)}, u32[]{:S(2)}, u32[]{:S(2)}) collective-permute-start(bf16[768,256]{1,0:T(8,128)(2,1)} %get-tuple-element.101), channel_id=1, source_target_pairs={{0,16},{8,24},{16,32},{24,40},{32,48},{40,56},{48,0},{56,8},{64,80... | collective-permute-start | bytes 1179656 | tf_op jit(solution)/shard_map/ppermute | solution.py:433
  175.0 15.3 %collective-permute-start.20 = (bf16[768,256]{1,0:T(8,128)(2,1)}, bf16[768,256]{1,0:T(8,128)(2,1)}, u32[]{:S(2)}, u32[]{:S(2)}) collective-permute-start(bf16[768,256]{1,0:T(8,128)(2,1)} %add_convert_fusion.1), channel_id=1, source_target_pairs={{0,64},{8,72},{16,80},{24,88},{32,96},{40,104},{48,112},{56,120},{... | collective-permute-start | bytes 1179656 | tf_op jit(solution)/shard_map/ppermute | solution.py:433
  178.6 14.0 %collective-permute-start.22 = (bf16[768,256]{1,0:T(8,128)(2,1)}, bf16[768,256]{1,0:T(8,128)(2,1)}, u32[]{:S(2)}, u32[]{:S(2)}) collective-permute-start(bf16[768,256]{1,0:T(8,128)(2,1)} %shard_map.150), channel_id=1, source_target_pairs={{0,64},{8,72},{16,80},{24,88},{32,96},{40,104},{48,112},{56,120},{... | collective-permute-start | bytes 1179656 | tf_op jit(solution)/shard_map/ppermute | solution.py:433
  182.8 18.4 %all-to-all-start.2 = ((bf16[16,96,128]{2,1,0:T(8,128)(2,1)}), bf16[16,96,128]{2,1,0:T(8,128)(2,1)S(1)}, u32[]{:S(2)}, u32[]{:S(2)}) async-start(bf16[16,96,128]{2,1,0:T(8,128)(2,1)} %get-tuple-element.81), calls=%async_computation.2 | async-start | bytes 786432 | tf_op jit(solution)/shard_map/all_to_all | solution.py:499
  (29 other events, 259.9 us)

commit v2 on v1

--- a/solution.py
+++ b/solution.py
@@ -51,7 +51,7 @@
 HBM = pl.BlockSpec(memory_space=pltpu.HBM)
 
 
-def call(kernel, out_shape, *args, smem=0, near=True, limit=None, scratch=(), far=(), dram=(), far_out=False):
+def call(kernel, out_shape, *args, smem=0, near=True, limit=None, scratch=(), far=(), dram=(), far_out=False, out_specs=None):
     outs = out_shape if isinstance(out_shape, (list, tuple)) else [out_shape]
     specs = [SMEM] * smem + [VMEM] * (len(args) - smem)
     for i in far:
@@ -67,7 +67,7 @@
         kernel,
         out_shape=out_shape,
         in_specs=specs,
-        out_specs=[out_spec] * len(outs) if isinstance(out_shape, (list, tuple)) else out_spec,
+        out_specs=out_specs or [out_spec] * len(outs) if isinstance(out_shape, (list, tuple)) else out_spec,
         scratch_shapes=list(scratch),
         compiler_params=params,
     )(*args)
@@ -237,25 +237,39 @@
             routed[:, (2 * n + c) * TOK : (2 * n + c + 1) * TOK] = router_rows(pieces[n], c)
 
 
-def output_kernel(i):
-    def kernel(rows, act, grad_gate, grad_up, first, last, *refs):
-        out, gain = refs[-2:]
-        some = slice(i * SLOTS, (i + 1) * SLOTS)
-        for b in range(CHIPS):
-            cols = slice(b * BK, (b + 1) * BK)
-            more = slice(D + b * BK, D + (b + 1) * BK)
-            piece = first.at[EARLY.index(b)] if b in EARLY else last.at[LATE.index(b)]
-            made = nt(act[some, :], piece[512:768, :])
-            total = nt(grad_gate[some, :], piece[0:256, :])
-            total = total + nt(grad_up[some, :], piece[256:512, :])
-            gain[:, cols] = jnp.sum(total * rows[:, cols].astype(F32), axis=0, keepdims=True)
-            if len(refs) == 3:
-                made = made + refs[0][:, cols].astype(F32)
-                total = total + refs[0][:, more].astype(F32)
-            out[:, cols] = made.astype(BF)
-            out[:, more] = total.astype(BF)
-
-    return kernel
+def output_kernel(rows, act, grad_gate, grad_up, first, last, *refs):
+    i = 1 if len(refs) == 2 else 0
+    some = slice(i * SLOTS, (i + 1) * SLOTS)
+    copies = []
+    if i == 0:
+        received, target, gain, out, sems = refs
+    else:
+        out, gain = refs
+    for b in range(CHIPS):
+        cols = slice(b * BK, (b + 1) * BK)
+        more = slice(D + b * BK, D + (b + 1) * BK)
+        piece = first.at[EARLY.index(b)] if b in EARLY else last.at[LATE.index(b)]
+        made = nt(act[some, :], piece[512:768, :])
+        total = nt(grad_gate[some, :], piece[0:256, :])
+        total = total + nt(grad_up[some, :], piece[256:512, :])
+        gain[:, cols] = jnp.sum(total * rows[:, cols].astype(F32), axis=0, keepdims=True)
+        if i == 0:
+            made = made + received[:, cols].astype(F32)
+            total = total + received[:, more].astype(F32)
+        out[:, cols] = made.astype(BF)
+        out[:, more] = total.astype(BF)
+        if i == 0 and b % 2:
+            for h, start in enumerate((0, D)):
+                span = slice(start + (b - 1) * BK, start + (b + 1) * BK)
+                copies.append(
+                    pltpu.make_async_copy(out.at[:, span], target.at[:, span], sems.at[b // 2, h])
+                )
+                copies[-1].start()
+    for c in copies:
+        c.wait()
+
+
+HALVED = (3, 5)
 
 
 def grads_kernel(blocks):
@@ -273,7 +287,7 @@
             stage[slot, 512:768, :] = nn(
                 flipped[D + b * BK : D + (b + 1) * BK, :], scaled[...]
             ).astype(BF)
-            if b == 3:
+            if b in HALVED:
                 copies[n] = [
                     pltpu.make_async_copy(stage.at[slot, :, side], out, sems.at[slot, h])
                     for h, (side, out) in enumerate(zip(SIDES, (outs[n], outs[-1])))
@@ -453,46 +467,20 @@
 
 def reduce_pieces(parts):
     across_2 = send(parts[6], BEHIND)
-    across_1 = send(parts[5], AHEAD)
+    across_1 = [send(v, AHEAD) for v in (parts[5], parts[9])]
     own_2 = send(parts[2], AHEAD)
     across_3 = [send(plus(parts[7][:, side], across_2[:, side]), BEHIND) for side in SIDES]
     own_3 = [send(v, BEHIND) for v in (parts[3], parts[8])]
     own_1 = [send(plus(parts[1][:, side], own_2[:, side]), AHEAD) for side in SIDES]
+    base, ahead = lax.optimization_barrier((parts[4], across_1[1]))
     across = [
         send(v, ACROSS)
         for v in (
-            plus(parts[4][:, LEFT], across_1[:, LEFT], across_3[0]),
-            plus_half(1, parts[4], across_1, across_3[1]),
+            plus(parts[4][:, LEFT], across_1[0], across_3[0]),
+            plus(base[:, RIGHT], ahead, across_3[1]),
         )
     ]
     return parts[0], *own_1, *own_3, *across
-
-
-def sum_kernel(h):
-    def kernel(*refs):
-        sources, out, stage, sems = refs[:-3], refs[-3], refs[-2], refs[-1]
-        copies = []
-        for n, source in enumerate(sources):
-            if source.shape[1] != BK:
-                source = source.at[:, h * BK : (h + 1) * BK]
-            copies.append(pltpu.make_async_copy(source, stage.at[n], sems.at[n]))
-            copies[n].start()
-        for c in copies:
-            c.wait()
-        total = stage[0].astype(F32)
-        for n in range(1, len(copies)):
-            total = total + stage[n].astype(F32)
-        out[...] = total.astype(BF)
-
-    return kernel
-
-
-def plus_half(h, *values):
-    count = len(values)
-    return call(
-        sum_kernel(h), sds((768, BK), BF), *values, far=range(count), limit=MiB(3),
-        scratch=[pltpu.VMEM((count, 768, BK), BF), pltpu.SemaphoreType.DMA((count,))],
-    )
 
 
 def exchange(v, axis):
@@ -550,22 +538,25 @@
     )
     shapes = [sds((SLOTS, 2 * D), BF), sds((1, D), F32)]
     operands = (act, grad_gate, grad_up, held_early, held_late)
-    partial, gain_other = call(output_kernel(1), shapes, rows_other, *operands, limit=MiB(6))
+    partial, gain_other = call(output_kernel, shapes, rows_other, *operands, limit=MiB(6))
     received = send(partial, SIBLING)
-    output, gain_mine = call(output_kernel(0), shapes, rows, *operands, received, limit=MiB(8))
+    output, gain_mine = call(
+        output_kernel, [pltpu.HBM((SLOTS, 2 * D), BF), sds((1, D), F32)],
+        rows, *operands, received, limit=MiB(8), out_specs=[HBM, VMEM],
+        scratch=[pltpu.VMEM((SLOTS, 2 * D), BF), pltpu.SemaphoreType.DMA((4, 2))],
+    )
     returned = exchange(output.reshape(WIN, CAP, 2 * D), "expert")
     returned = returned.reshape(SLOTS, 2 * D)
     parts = {}
-    for blocks in ((6, 5, 2), (3, 7, 1, 4, 0)):
-        shapes = [pltpu.HBM((768, BK if b == 3 else HALF), BF) for b in blocks]
-        if 3 in blocks:
-            shapes.append(pltpu.HBM((768, BK), BF))
+    for blocks, extra in (((6, 5, 2), 9), ((3, 7, 1, 4, 0), 8)):
+        shapes = [pltpu.HBM((768, BK if b in HALVED else HALF), BF) for b in blocks]
+        shapes.append(pltpu.HBM((768, BK), BF))
         made = call(
             grads_kernel(blocks), shapes, flipped, scaled, grad_gate, grad_up,
             limit=MiB(5), far_out=True,
             scratch=[pltpu.VMEM((3, 768, HALF), BF), pltpu.SemaphoreType.DMA((3, 2))],
         )
-        parts.update(zip(blocks + (8,), made))
+        parts.update(zip(blocks + (extra,), made))
     give, keep = call(
         total_kernel, [sds((384, HALF), BF)] * 2, place, *reduce_pieces(parts),
         smem=1, limit=MiB(6),

time: 216 us -> 216 us (level)
    unnamed x51 -> x47, local copies, waits for them, and re-layouts: 11.4 us -> 9.64 us
    ppermute x24 -> x25, starting transfers between devices: 32.7 us -> 34.3 us  [send(): return lax.ppermute(v, DP, pairs)]
    pallas_call x18 -> x17, Pallas kernels: 42.8 us -> 41.3 us  [call(): pl.pallas_call(kernel, out_shape=out_shape, in_specs=specs, out_specs=out...]
    ppermute x24 -> x25, waiting for transfers between devices: 72.9 us -> 74.1 us  [send(): return lax.ppermute(v, DP, pairs)]
    convert_element_type x3 -> x4, other arithmetic: 3.72 us -> 4.55 us  [plus(): return total.astype(BF)]
  transfers between devices with their start and end apart: 28 -> 29, of which waited for: 11 -> 11; matrix products, arithmetic and copies ran while one was open for 2% -> 2% of each run, Pallas kernels for 15% -> 14%
where the time goes in v2:
time: 216 us; the launch traced here: 215 us
  waiting for transfers between devices  102 us (47%)
  starting transfers between devices  56.1 us (26%)
  Pallas kernels  41.3 us (19%)
  local copies, waits for them, and re-layouts  9.7 us (4%)
  other arithmetic  4.55 us (2%)
    ppermute x25, waiting for transfers between devices, send(): return lax.ppermute(v, DP, pairs)  74.1 us
    pallas_call x17, Pallas kernels, call(): pl.pallas_call(kernel, out_shape=out_shape, in_specs=specs, out_specs=out...  41.3 us
    ppermute x25, starting transfers between devices, send(): return lax.ppermute(v, DP, pairs)  34.3 us
    all_to_all x4, waiting for transfers between devices, exchange(): return lax.all_to_all(v, axis, split_axis=0, concat_axis=0, tiled=True)  27.9 us
    all_to_all x4, starting transfers between devices, exchange(): return lax.all_to_all(v, axis, split_axis=0, concat_axis=0, tiled=True)  21.8 us
    unnamed x47, local copies, waits for them, and re-layouts  9.64 us
    convert_element_type x4, other arithmetic, plus(): return total.astype(BF)  4.55 us
  transfers between devices with their start and end apart: 29, of which 11 were waited for; matrix products, arithmetic and copies ran while one was open for 2% of the time, Pallas kernels for 14%

profile of v2, /device:TPU:1, one launch (start us, length us, event | category | flops | bytes accessed | tf_op | source)
XLA Modules:
  0.0 214.8 jit_solution(16463942972590165288)
XLA Ops:
  1.4 4.0 %shard_map.135 = (bf16[128,2048]{1,0:T(8,128)(2,1)}, bf16[128,2048]{1,0:T(8,128)(2,1)}, f32[1,2048]{1,0:T(1,128)}, f32[128,128]{1,0:T(8,128)}, bf16[128,256]{1,0...) custom-call(s32[16]{0:T(128)S(1)} %compare_select_fusion.1.place, bf16[128,2048]{1,0:T(8,128)(2,1)} %tokens.1, ...), custom_call_target="tpu_custom_call" | custom-call | tf_op jit(solution)/shard_map/pallas_call | solution.py:66
  5.4 7.5 %all-to-all-start = ((bf16[8,32,4224]{2,1,0:T(8,128)(2,1)}), bf16[8,32,4224]{2,1,0:T(8,128)(2,1)S(1)}, u32[]{:S(2)}, u32[]{:S(2)}) async-start(bf16[8,32,4224]{2,1,0:T(8,128)(2,1)} %bitcast.21), calls=%async_computation | async-start | bytes 4325376 | tf_op jit(solution)/shard_map/all_to_all | solution.py:487
  15.9 25.2 %all-to-all-done = bf16[8,32,4224]{2,1,0:T(8,128)(2,1)S(1)} async-done(((bf16[8,32,4224]{2,1,0:T(8,128)(2,1)}), bf16[8,32,4224]{2,1,0:T(8,128)(2,1)S(1)}, u32[]{:S(2)}, u32[]{:S(2)}) %all-to-all-start) | async-done | bytes 2162720 | tf_op jit(solution)/shard_map/all_to_all | solution.py:487
  47.9 18.2 %collective-permute-done.2.refs_2_ = bf16[800,512]{1,0:T(8,128)(2,1)S(1)} collective-permute-done((bf16[800,512]{1,0:T(8,128)(2,1)S(1)}, bf16[800,512]{1,0:T(8,128)(2,1)S(1)}, u32[]{:S(2)}, u32[]{:S(2)}) %collective-permute-start.2) | collective-permute-done | bytes 819232 | tf_op jit(solution)/shard_map/ppermute | solution.py:447
  71.6 5.3 %collective-permute-done.5.refs_5_ = bf16[800,256]{1,0:T(8,128)(2,1)S(1)} collective-permute-done((bf16[800,256]{1,0:T(8,128)(2,1)S(1)}, bf16[800,256]{1,0:T(8,128)(2,1)S(1)}, u32[]{:S(2)}, u32[]{:S(2)}) %collective-permute-start.5) | collective-permute-done | bytes 409632 | tf_op jit(solution)/shard_map/ppermute | solution.py:447
  76.9 3.4 %collective-permute-start.9 = (bf16[800,256]{1,0:T(8,128)(2,1)S(1)}, bf16[800,256]{1,0:T(8,128)(2,1)S(1)}, u32[]{:S(2)}, u32[]{:S(2)}) collective-permute-start(bf16[800,256]{1,0:T(8,128)(2,1)S(1)} %collective-permute-done.5.refs_5_), channel_id=1, source_target_pairs={{0,48},{8,56},{16,0},{24,8},{32,16},{40,24},{48,32},{56,40},{64,11... | collective-permute-start | bytes 1228808 | tf_op jit(solution)/shard_map/ppermute | solution.py:447
  80.3 5.4 %collective-permute-done.6.refs_6_ = bf16[800,256]{1,0:T(8,128)(2,1)S(1)} collective-permute-done((bf16[800,256]{1,0:T(8,128)(2,1)S(1)}, bf16[800,256]{1,0:T(8,128)(2,1)S(1)}, u32[]{:S(2)}, u32[]{:S(2)}) %collective-permute-start.6) | collective-permute-done | bytes 409632 | tf_op jit(solution)/shard_map/ppermute | solution.py:447
  85.7 3.4 %collective-permute-start.10 = (bf16[800,256]{1,0:T(8,128)(2,1)S(1)}, bf16[800,256]{1,0:T(8,128)(2,1)S(1)}, u32[]{:S(2)}, u32[]{:S(2)}) collective-permute-start(bf16[800,256]{1,0:T(8,128)(2,1)S(1)} %collective-permute-done.6.refs_6_), channel_id=1, source_target_pairs={{0,48},{8,56},{16,0},{24,8},{32,16},{40,24},{48,32},{56,40},{64,11... | collective-permute-start | bytes 1228808 | tf_op jit(solution)/shard_map/ppermute | solution.py:447
  90.0 4.7 %shard_map.138 = (f32[256,1536]{1,0:T(8,128)S(1)}, f32[256,64]{1,0:T(8,128)S(1)}, bf16[64,1536]{1,0:T(8,128)(2,1)}, bf16[6,800,512]{2,1,0:T(8,128)(2,1)S(1)}) custom-call(bf16[256,4224]{1,0:T(8,128)(2,1)S(1)} %bitcast.15, bf16[800,512]{1,0:T(8,128)(2,1)} %copy-done.2, bf16[800,512]{1,0:T(8,128)(2,1)} %copy-done.13, bf16[800,512]{1,0:T(8,128)(2,1)} %copy-done.11, ...), custom_call_target="tpu_custom_call" | custom-call | tf_op jit(solution)/shard_map/pallas_call | solution.py:66
  96.3 7.8 %collective-permute-done.8.refs_6_ = bf16[800,512]{1,0:T(8,128)(2,1)S(1)} collective-permute-done((bf16[800,512]{1,0:T(8,128)(2,1)S(1)}, bf16[800,512]{1,0:T(8,128)(2,1)S(1)}, u32[]{:S(2)}, u32[]{:S(2)}) %collective-permute-start.8) | collective-permute-done | bytes 819232 | tf_op jit(solution)/shard_map/ppermute | solution.py:447
  105.3 4.3 %shard_map.140 = (bf16[512,512]{1,0:T(8,128)(2,1)S(1)}, bf16[512,512]{1,0:T(8,128)(2,1)S(1)}, bf16[512,512]{1,0:T(8,128)(2,1)S(1)}, bf16[512,512]{1,0:T(8,128)(2...) custom-call(s32[16]{0:T(128)S(1)} %compare_select_fusion.1.place, bf16[256,4224]{1,0:T(8,128)(2,1)S(1)} %bitcast.16, ...), custom_call_target="tpu_custom_call" | custom-call | tf_op jit(solution)/shard_map/pallas_call | solution.py:66
  122.4 3.6 %all-to-all-start.1 = ((bf16[8,32,4096]{2,1,0:T(8,128)(2,1)}), bf16[8,32,4096]{2,1,0:T(8,128)(2,1)S(1)}, u32[]{:S(2)}, u32[]{:S(2)}) async-start(bf16[8,32,4096]{2,1,0:T(8,128)(2,1)} %bitcast.22), calls=%async_computation.1 | async-start | bytes 4194304 | tf_op jit(solution)/shard_map/all_to_all | solution.py:487
  129.4 3.6 %shard_map.148 = (bf16[768,256]{1,0:T(8,128)(2,1)}, bf16[768,512]{1,0:T(8,128)(2,1)}, bf16[768,512]{1,0:T(8,128)(2,1)}, bf16[768,512]{1,0:T(8,128)(2,1)}, bf16[7...) custom-call(bf16[4096,512]{1,0:T(8,128)(2,1)S(1)} %copy-done.1, bf16[512,512]{1,0:T(8,128)(2,1)S(1)} %copy-done.4, ...), custom_call_target="tpu_custom_call" | custom-call | tf_op jit(solution)/shard_map/pallas_call | solution.py:66
  133.9 2.9 %collective-permute-done.18 = bf16[768,512]{1,0:T(8,128)(2,1)} collective-permute-done((bf16[768,512]{1,0:T(8,128)(2,1)}, bf16[768,512]{1,0:T(8,128)(2,1)}, u32[]{:S(2)}, u32[]{:S(2)}) %collective-permute-start.18) | collective-permute-done | bytes 786464 | tf_op jit(solution)/shard_map/ppermute | solution.py:447
  138.5 3.5 %collective-permute-start.19 = (bf16[768,256]{1,0:T(8,128)(2,1)S(1)}, bf16[768,256]{1,0:T(8,128)(2,1)S(1)}, u32[]{:S(2)}, u32[]{:S(2)}) collective-permute-start(bf16[768,256]{1,0:T(8,128)(2,1)S(1)} %get-tuple-element.106), channel_id=1, source_target_pairs={{0,48},{8,56},{16,0},{24,8},{32,16},{40,24},{48,32},{56,40},{64,11... | collective-permute-start | bytes 1179656 | tf_op jit(solution)/shard_map/ppermute | solution.py:447
  142.0 12.7 %collective-permute-done.21 = bf16[768,256]{1,0:T(8,128)(2,1)S(1)} collective-permute-done((bf16[768,256]{1,0:T(8,128)(2,1)}, bf16[768,256]{1,0:T(8,128)(2,1)S(1)}, u32[]{:S(2)}, u32[]{:S(2)}) %collective-permute-start.21) | collective-permute-done | bytes 393248 | tf_op jit(solution)/shard_map/ppermute | solution.py:447
  155.9 7.3 %collective-permute-done.17 = bf16[768,256]{1,0:T(8,128)(2,1)S(1)} collective-permute-done((bf16[768,256]{1,0:T(8,128)(2,1)S(1)}, bf16[768,256]{1,0:T(8,128)(2,1)S(1)}, u32[]{:S(2)}, u32[]{:S(2)}) %collective-permute-start.17) | collective-permute-done | bytes 393248 | tf_op jit(solution)/shard_map/ppermute | solution.py:447
  164.1 10.7 %collective-permute-done.22 = bf16[768,256]{1,0:T(8,128)(2,1)S(1)} collective-permute-done((bf16[768,256]{1,0:T(8,128)(2,1)S(1)}, bf16[768,256]{1,0:T(8,128)(2,1)S(1)}, u32[]{:S(2)}, u32[]{:S(2)}) %collective-permute-start.22) | collective-permute-done | bytes 393248 | tf_op jit(solution)/shard_map/ppermute | solution.py:447
  178.0 3.5 %shard_map.143 = (f32[128,64]{1,0:T(8,128)S(1)}, f32[128,64]{1,0:T(8,128)S(1)}, bf16[16,96,128]{2,1,0:T(8,128)(2,1)}) custom-call(s32[16]{0:T(128)S(1)} %compare_select_fusion.1.place, bf16[256,4096]{1,0:T(8,128)(2,1)S(1)} %bitcast.19, bf16[128,2048]{1,0:T(8,128)(2,1)} %cotangent.3, bf16[128,256]{1,0:T(8,128)(2,1)} %get-tuple-element.70.spread, ...), custom_call_target="tpu_custom_call" | custom-call | tf_op jit(solution)/shard_map/pallas_call | solution.py:66
  181.5 7.3 %all-to-all-start.2 = ((bf16[16,96,128]{2,1,0:T(8,128)(2,1)}), bf16[16,96,128]{2,1,0:T(8,128)(2,1)S(1)}, u32[]{:S(2)}, u32[]{:S(2)}) async-start(bf16[16,96,128]{2,1,0:T(8,128)(2,1)} %get-tuple-element.84), calls=%async_computation.2 | async-start | bytes 786432 | tf_op jit(solution)/shard_map/all_to_all | solution.py:487
  188.8 3.7 %collective-permute-done.23.refs_5_ = bf16[768,256]{1,0:T(8,128)(2,1)} collective-permute-done((bf16[768,256]{1,0:T(8,128)(2,1)}, bf16[768,256]{1,0:T(8,128)(2,1)}, u32[]{:S(2)}, u32[]{:S(2)}) %collective-permute-start.23) | collective-permute-done | bytes 393248 | tf_op jit(solution)/shard_map/ppermute | solution.py:447
  196.8 4.7 %collective-permute-start.24 = (bf16[384,512]{1,0:T(8,128)(2,1)}, bf16[384,512]{1,0:T(8,128)(2,1)S(1)}, u32[]{:S(2)}, u32[]{:S(2)}) collective-permute-start(bf16[384,512]{1,0:T(8,128)(2,1)} %get-tuple-element.101), channel_id=1, source_target_pairs={{0,8},{8,0},{16,24},{24,16},{32,40},{40,32},{48,56},{56,48},{64,72... | collective-permute-start | bytes 1179656 | tf_op jit(solution)/shard_map/ppermute | solution.py:447
  202.3 3.4 %all-to-all-start.3 = ((f32[8,80,128]{2,1,0:T(8,128)}), f32[8,80,128]{2,1,0:T(8,128)S(1)}, u32[]{:S(2)}, u32[]{:S(2)}) async-start(f32[8,80,128]{2,1,0:T(8,128)} %shard_map.145), calls=%async_computation.3 | async-start | bytes 655360 | tf_op jit(solution)/shard_map/all_to_all | solution.py:487
  208.2 3.2 %shard_map.144 = (bf16[128,2048]{1,0:T(8,128)(2,1)}, bf16[128,2048]{1,0:T(8,128)(2,1)}) custom-call(s32[16]{0:T(128)S(1)} %compare_select_fusion.1.place, bf16[256,4096]{1,0:T(8,128)(2,1)S(1)} %bitcast.20, bf16[128,256]{1,0:T(8,128)(2,1)} %get-tuple-element.70.spread, f32[128,64]{1,0:T(8,128)S(1)} %get-tuple-element.78.weight, ...), custom_call_target="tpu_custom_call" | custom-call | tf_op jit(solution)/shard_map/pallas_call | solution.py:66
  (104 shorter events, 54.4 us)
Async XLA Ops:
  5.4 35.7 %all-to-all-start = ((bf16[8,32,4224]{2,1,0:T(8,128)(2,1)}), bf16[8,32,4224]{2,1,0:T(8,128)(2,1)S(1)}, u32[]{:S(2)}, u32[]{:S(2)}) async-start(bf16[8,32,4224]{2,1,0:T(8,128)(2,1)} %bitcast.21), calls=%async_computation | async-start | bytes 4325376 | tf_op jit(solution)/shard_map/all_to_all | solution.py:487
  14.9 28.1 %collective-permute-start = (bf16[400,512]{1,0:T(8,128)(2,1)S(1)}, bf16[400,512]{1,0:T(8,128)(2,1)S(1)}, u32[]{:S(2)}, u32[]{:S(2)}) collective-permute-start(bf16[400,512]{1,0:T(8,128)(2,1)S(1)} %get-tuple-element.58), channel_id=1, source_target_pairs={{0,8},{8,0},{16,24},{24,16},{32,40},{40,32},{48,56},{56,48},{64,72... | collective-permute-start | bytes 1228808 | tf_op jit(solution)/shard_map/ppermute | solution.py:447
  41.2 53.5 %collective-permute-start.7 = (bf16[256,4224]{1,0:T(8,128)(2,1)S(1)}, bf16[256,4224]{1,0:T(8,128)(2,1)S(1)}, u32[]{:S(2)}, u32[]{:S(2)}) collective-permute-start(bf16[256,4224]{1,0:T(8,128)(2,1)S(1)} %bitcast.14), channel_id=1, source_target_pairs={{0,8},{8,0},{16,24},{24,16},{32,40},{40,32},{48,56},{56,48},{64,72... | collective-permute-start | bytes 6488072 | tf_op jit(solution)/shard_map/ppermute | solution.py:447
  43.7 22.4 %collective-permute-start.2 = (bf16[800,512]{1,0:T(8,128)(2,1)S(1)}, bf16[800,512]{1,0:T(8,128)(2,1)S(1)}, u32[]{:S(2)}, u32[]{:S(2)}) collective-permute-start(bf16[800,512]{1,0:T(8,128)(2,1)S(1)} %shard_map.137.refs_0_), channel_id=1, source_target_pairs={{0,16},{8,24},{16,32},{24,40},{32,48},{40,56},{48,0},{56,8},{64,80... | collective-permute-start | bytes 2457608 | tf_op jit(solution)/shard_map/ppermute | solution.py:447
  45.4 20.7 %collective-permute-start.3 = (bf16[800,512]{1,0:T(8,128)(2,1)S(1)}, bf16[800,512]{1,0:T(8,128)(2,1)S(1)}, u32[]{:S(2)}, u32[]{:S(2)}) collective-permute-start(bf16[800,512]{1,0:T(8,128)(2,1)S(1)} %shard_map.137.refs_0_), channel_id=1, source_target_pairs={{0,64},{8,72},{16,80},{24,88},{32,96},{40,104},{48,112},{56,120},{... | collective-permute-start | bytes 2457608 | tf_op jit(solution)/shard_map/ppermute | solution.py:447
  45.7 23.2 %collective-permute-start.1 = (bf16[800,512]{1,0:T(8,128)(2,1)S(1)}, bf16[800,512]{1,0:T(8,128)(2,1)S(1)}, u32[]{:S(2)}, u32[]{:S(2)}) collective-permute-start(bf16[800,512]{1,0:T(8,128)(2,1)S(1)} %shard_map.137.refs_0_), channel_id=1, source_target_pairs={{0,48},{8,56},{16,0},{24,8},{32,16},{40,24},{48,32},{56,40},{64,11... | collective-permute-start | bytes 2457608 | tf_op jit(solution)/shard_map/ppermute | solution.py:447
  66.1 23.0 %collective-permute-start.4 = (bf16[800,512]{1,0:T(8,128)(2,1)S(1)}, bf16[800,512]{1,0:T(8,128)(2,1)S(1)}, u32[]{:S(2)}, u32[]{:S(2)}) collective-permute-start(bf16[800,512]{1,0:T(8,128)(2,1)S(1)} %collective-permute-done.2.refs_2_), channel_id=1, source_target_pairs={{0,16},{8,24},{16,32},{24,40},{32,48},{40,56},{48,0},{56,8},{64,80... | collective-permute-start | bytes 2457608 | tf_op jit(solution)/shard_map/ppermute | solution.py:447
  68.9 35.2 %collective-permute-start.8 = (bf16[800,512]{1,0:T(8,128)(2,1)S(1)}, bf16[800,512]{1,0:T(8,128)(2,1)S(1)}, u32[]{:S(2)}, u32[]{:S(2)}) collective-permute-start(bf16[800,512]{1,0:T(8,128)(2,1)S(1)} %collective-permute-done.3.refs_3_), channel_id=1, source_target_pairs={{0,16},{8,24},{16,32},{24,40},{32,48},{40,56},{48,0},{56,8},{64,80... | collective-permute-start | bytes 2457608 | tf_op jit(solution)/shard_map/ppermute | solution.py:447
  68.9 16.7 %collective-permute-start.6 = (bf16[800,256]{1,0:T(8,128)(2,1)S(1)}, bf16[800,256]{1,0:T(8,128)(2,1)S(1)}, u32[]{:S(2)}, u32[]{:S(2)}) collective-permute-start(bf16[800,256]{1,0:T(8,128)(2,1)S(1)} %get-tuple-element.109), channel_id=1, source_target_pairs={{0,48},{8,56},{16,0},{24,8},{32,16},{40,24},{48,32},{56,40},{64,11... | collective-permute-start | bytes 1228808 | tf_op jit(solution)/shard_map/ppermute | solution.py:447
  76.9 27.2 %collective-permute-start.9 = (bf16[800,256]{1,0:T(8,128)(2,1)S(1)}, bf16[800,256]{1,0:T(8,128)(2,1)S(1)}, u32[]{:S(2)}, u32[]{:S(2)}) collective-permute-start(bf16[800,256]{1,0:T(8,128)(2,1)S(1)} %collective-permute-done.5.refs_5_), channel_id=1, source_target_pairs={{0,48},{8,56},{16,0},{24,8},{32,16},{40,24},{48,32},{56,40},{64,11... | collective-permute-start | bytes 1228808 | tf_op jit(solution)/shard_map/ppermute | solution.py:447
  85.7 18.4 %collective-permute-start.10 = (bf16[800,256]{1,0:T(8,128)(2,1)S(1)}, bf16[800,256]{1,0:T(8,128)(2,1)S(1)}, u32[]{:S(2)}, u32[]{:S(2)}) collective-permute-start(bf16[800,256]{1,0:T(8,128)(2,1)S(1)} %collective-permute-done.6.refs_6_), channel_id=1, source_target_pairs={{0,48},{8,56},{16,0},{24,8},{32,16},{40,24},{48,32},{56,40},{64,11... | collective-permute-start | bytes 1228808 | tf_op jit(solution)/shard_map/ppermute | solution.py:447
  117.2 19.7 %collective-permute-start.18 = (bf16[768,512]{1,0:T(8,128)(2,1)}, bf16[768,512]{1,0:T(8,128)(2,1)}, u32[]{:S(2)}, u32[]{:S(2)}) collective-permute-start(bf16[768,512]{1,0:T(8,128)(2,1)} %get-tuple-element.96), channel_id=1, source_target_pairs={{0,48},{8,56},{16,0},{24,8},{32,16},{40,24},{48,32},{56,40},{64,11... | collective-permute-start | bytes 2359304 | tf_op jit(solution)/shard_map/ppermute | solution.py:447
  122.4 55.6 %all-to-all-start.1 = ((bf16[8,32,4096]{2,1,0:T(8,128)(2,1)}), bf16[8,32,4096]{2,1,0:T(8,128)(2,1)S(1)}, u32[]{:S(2)}, u32[]{:S(2)}) async-start(bf16[8,32,4096]{2,1,0:T(8,128)(2,1)} %bitcast.22), calls=%async_computation.1 | async-start | bytes 4194304 | tf_op jit(solution)/shard_map/all_to_all | solution.py:487
  126.0 28.7 %collective-permute-start.12 = (bf16[768,512]{1,0:T(8,128)(2,1)}, bf16[768,512]{1,0:T(8,128)(2,1)S(1)}, u32[]{:S(2)}, u32[]{:S(2)}) collective-permute-start(bf16[768,512]{1,0:T(8,128)(2,1)} %get-tuple-element.90), channel_id=1, source_target_pairs={{0,16},{8,24},{16,32},{24,40},{32,48},{40,56},{48,0},{56,8},{64,80... | collective-permute-start | bytes 2359304 | tf_op jit(solution)/shard_map/ppermute | solution.py:447
  126.1 28.6 %collective-permute-start.21 = (bf16[768,256]{1,0:T(8,128)(2,1)}, bf16[768,256]{1,0:T(8,128)(2,1)S(1)}, u32[]{:S(2)}, u32[]{:S(2)}) collective-permute-start(bf16[768,256]{1,0:T(8,128)(2,1)} %get-tuple-element.97), channel_id=1, source_target_pairs={{0,16},{8,24},{16,32},{24,40},{32,48},{40,56},{48,0},{56,8},{64,80... | collective-permute-start | bytes 1179656 | tf_op jit(solution)/shard_map/ppermute | solution.py:447
  133.0 30.1 %collective-permute-start.17 = (bf16[768,256]{1,0:T(8,128)(2,1)S(1)}, bf16[768,256]{1,0:T(8,128)(2,1)S(1)}, u32[]{:S(2)}, u32[]{:S(2)}) collective-permute-start(bf16[768,256]{1,0:T(8,128)(2,1)S(1)} %copy-done.21), channel_id=1, source_target_pairs={{0,16},{8,24},{16,32},{24,40},{32,48},{40,56},{48,0},{56,8},{64,80... | collective-permute-start | bytes 1179656 | tf_op jit(solution)/shard_map/ppermute | solution.py:447
  138.5 24.7 %collective-permute-start.19 = (bf16[768,256]{1,0:T(8,128)(2,1)S(1)}, bf16[768,256]{1,0:T(8,128)(2,1)S(1)}, u32[]{:S(2)}, u32[]{:S(2)}) collective-permute-start(bf16[768,256]{1,0:T(8,128)(2,1)S(1)} %get-tuple-element.106), channel_id=1, source_target_pairs={{0,48},{8,56},{16,0},{24,8},{32,16},{40,24},{48,32},{56,40},{64,11... | collective-permute-start | bytes 1179656 | tf_op jit(solution)/shard_map/ppermute | solution.py:447
  141.9 34.2 %collective-permute-start.15 = (bf16[768,256]{1,0:T(8,128)(2,1)S(1)}, bf16[768,256]{1,0:T(8,128)(2,1)S(1)}, u32[]{:S(2)}, u32[]{:S(2)}) collective-permute-start(bf16[768,256]{1,0:T(8,128)(2,1)S(1)} %copy-done.22), channel_id=1, source_target_pairs={{0,48},{8,56},{16,0},{24,8},{32,16},{40,24},{48,32},{56,40},{64,11... | collective-permute-start | bytes 1179656 | tf_op jit(solution)/shard_map/ppermute | solution.py:447
  154.8 34.0 %collective-permute-start.16 = (bf16[768,256]{1,0:T(8,128)(2,1)}, bf16[768,256]{1,0:T(8,128)(2,1)}, u32[]{:S(2)}, u32[]{:S(2)}) collective-permute-start(bf16[768,256]{1,0:T(8,128)(2,1)} %get-tuple-element.92), channel_id=1, source_target_pairs={{0,48},{8,56},{16,0},{24,8},{32,16},{40,24},{48,32},{56,40},{64,11... | collective-permute-start | bytes 1179656 | tf_op jit(solution)/shard_map/ppermute | solution.py:447
  154.8 20.1 %collective-permute-start.22 = (bf16[768,256]{1,0:T(8,128)(2,1)S(1)}, bf16[768,256]{1,0:T(8,128)(2,1)S(1)}, u32[]{:S(2)}, u32[]{:S(2)}) collective-permute-start(bf16[768,256]{1,0:T(8,128)(2,1)S(1)} %get-tuple-element.105), channel_id=1, source_target_pairs={{0,48},{8,56},{16,0},{24,8},{32,16},{40,24},{48,32},{56,40},{64,11... | collective-permute-start | bytes 1179656 | tf_op jit(solution)/shard_map/ppermute | solution.py:447
  163.2 25.6 %collective-permute-start.13 = (bf16[768,256]{1,0:T(8,128)(2,1)}, bf16[768,256]{1,0:T(8,128)(2,1)}, u32[]{:S(2)}, u32[]{:S(2)}) collective-permute-start(bf16[768,256]{1,0:T(8,128)(2,1)} %get-tuple-element.108), channel_id=1, source_target_pairs={{0,16},{8,24},{16,32},{24,40},{32,48},{40,56},{48,0},{56,8},{64,80... | collective-permute-start | bytes 1179656 | tf_op jit(solution)/shard_map/ppermute | solution.py:447
  163.2 25.6 %collective-permute-start.14 = (bf16[768,256]{1,0:T(8,128)(2,1)}, bf16[768,256]{1,0:T(8,128)(2,1)}, u32[]{:S(2)}, u32[]{:S(2)}) collective-permute-start(bf16[768,256]{1,0:T(8,128)(2,1)} %get-tuple-element.107), channel_id=1, source_target_pairs={{0,16},{8,24},{16,32},{24,40},{32,48},{40,56},{48,0},{56,8},{64,80... | collective-permute-start | bytes 1179656 | tf_op jit(solution)/shard_map/ppermute | solution.py:447
  176.8 15.7 %collective-permute-start.23 = (bf16[768,256]{1,0:T(8,128)(2,1)}, bf16[768,256]{1,0:T(8,128)(2,1)}, u32[]{:S(2)}, u32[]{:S(2)}) collective-permute-start(bf16[768,256]{1,0:T(8,128)(2,1)} %add_convert_fusion), channel_id=1, source_target_pairs={{0,64},{8,72},{16,80},{24,88},{32,96},{40,104},{48,112},{56,120},{... | collective-permute-start | bytes 1179656 | tf_op jit(solution)/shard_map/ppermute | solution.py:447
  181.5 20.1 %all-to-all-start.2 = ((bf16[16,96,128]{2,1,0:T(8,128)(2,1)}), bf16[16,96,128]{2,1,0:T(8,128)(2,1)S(1)}, u32[]{:S(2)}, u32[]{:S(2)}) async-start(bf16[16,96,128]{2,1,0:T(8,128)(2,1)} %get-tuple-element.84), calls=%async_computation.2 | async-start | bytes 786432 | tf_op jit(solution)/shard_map/all_to_all | solution.py:487
  (28 other events, 274.3 us)
